TPU v7x, 32 devices: a whole 2x2x4 slice. The times are simulated.
32 devices in a mesh: batch: 2 (over x), cy: 4 (over z), cx: 4 (over y, core).
Axes of the slice: x: 2, y: 2, z: 4, core: 2. Of those that a mesh axis runs over, the one named last changes fastest.
Arguments:
- q: bfloat16 [16384, 24, 128], P(('batch', 'cy', 'cx')), parts along dimension 0
- k: bfloat16 [16384, 8, 128], P(('batch', 'cy', 'cx')), parts along dimension 0
- v: bfloat16 [16384, 8, 128], P(('batch', 'cy', 'cx')), parts along dimension 0
Outputs:
- output: bfloat16 [16384, 24, 128], P(('batch', 'cy', 'cx')), parts along dimension 0
There are 2 independent parts. A program takes and returns all parts, laid end to end along the dimension named above; each array names one.
All inputs are finite; a program needn't handle non-finite values.
Results may differ from a plain program's by a relative error of at most 0.00183193.
Values are sent between devices in bfloat16 or wider.
A program may use at most 1 GiB of HBM per device.

v0:
```python
import jax
import jax.numpy as jnp
from jax import lax
from jax.sharding import PartitionSpec as P

NEG = -1e30


def softmax_first(s, vb):
    m = jnp.max(s, axis=-1)
    p = jnp.exp(s - m[..., None])
    acc = jnp.einsum('kgqs,skd->kgqd', p.astype(jnp.bfloat16), vb, preferred_element_type=jnp.float32)
    return (m, jnp.sum(p, axis=-1), acc)


def softmax_step(m, l, acc, s, vb):
    m_new = jnp.maximum(m, jnp.max(s, axis=-1))
    alpha = jnp.exp(m - m_new)
    p = jnp.exp(s - m_new[..., None])
    l = l * alpha + jnp.sum(p, axis=-1)
    acc = acc * alpha[..., None] + jnp.einsum('kgqs,skd->kgqd', p.astype(jnp.bfloat16), vb, preferred_element_type=jnp.float32)
    return (m_new, l, acc)


def solution(mesh):
    nx = mesh.shape['cx']
    n = mesh.shape['cy'] * nx
    spec = P(('batch', 'cy', 'cx'), None, None)
    perm = [(i, (i + 1) % n) for i in range(n)]

    def local(q, k, v):
        t, h, d = q.shape
        kvh = k.shape[1]
        g = h // kvh
        c = t // 2
        scale = d ** -0.5
        r = lax.axis_index('cy') * nx + lax.axis_index('cx')
        qt = jnp.transpose(q.reshape(t, kvh, g, d), (1, 2, 0, 3))
        ql, qh = qt[:, :, :c], qt[:, :, c:]
        i = jnp.arange(c)
        tril = i[None, :] <= i[:, None]
        band = jnp.arange(t)[None, :] <= (i + c)[:, None]

        def scores(qx, kx):
            return jnp.einsum('kgqd,skd->kgqs', qx, kx, preferred_element_type=jnp.float32) * scale

        lo = softmax_first(jnp.where(tril, scores(ql, k[:c]), -jnp.inf), v[:c])
        hi = softmax_first(jnp.where(band, scores(qh, k), -jnp.inf), v)

        def lower(st, kb, vb):
            lo, hi = st
            kl, vl = kb[:c], vb[:c]
            return (softmax_step(*lo, scores(ql, kl), vl), softmax_step(*hi, scores(qh, kl), vl))

        def higher(st, kb, vb):
            lo, hi = st
            return (lo, softmax_step(*hi, scores(qh, kb), vb))

        state = (lo, hi)
        kb = k
        vb = v
        for step in range(1, n):
            kb = lax.ppermute(kb, ('cy', 'cx'), perm)
            vb = lax.ppermute(vb, ('cy', 'cx'), perm)
            state = lax.cond(step <= r, lower, higher, state, kb, vb)
        lo, hi = state
        o = jnp.concatenate([lo[2] / lo[1][..., None], hi[2] / hi[1][..., None]], axis=2)
        return jnp.transpose(o, (2, 0, 1, 3)).reshape(t, h, d).astype(jnp.bfloat16)

    return jax.shard_map(local, mesh=mesh, in_specs=(spec, spec, spec), out_specs=spec, check_vma=False)
```

profile of v0, /device:TPU:31, one launch (start us, length us, event | category | flops | bytes accessed | tf_op | source)
XLA Modules:
  0.0 511.3 jit_solution(16712041475069162568)
XLA Ops:
  3.4 10.3 %collective-permute-done = bf16[512,8,128]{2,0,1:T(8,128)(2,1)S(1)} collective-permute-done((bf16[512,8,128]{2,0,1:T(8,128)(2,1)S(1)}, bf16[512,8,128]{2,0,1:T(8,128)(2,1)S(1)}, u32[]{:S(2)}, u32[]{:S(2)}) %collective-permute-start) | collective-permute-done | bytes 1048608 | tf_op jit(solution)/shard_map/ppermute | solution.py:63
  18.9 6.0 %collective-permute-done.15 = bf16[512,8,128]{2,0,1:T(8,128)(2,1)S(1)} collective-permute-done((bf16[512,8,128]{2,0,1:T(8,128)(2,1)S(1)}, bf16[512,8,128]{2,0,1:T(8,128)(2,1)S(1)}, u32[]{:S(2)}, u32[]{:S(2)}) %collective-permute-start.15) | collective-permute-done | bytes 1048608 | tf_op jit(solution)/shard_map/ppermute | solution.py:64
  30.2 6.0 %collective-permute-done.1 = bf16[512,8,128]{2,0,1:T(8,128)(2,1)S(1)} collective-permute-done((bf16[512,8,128]{2,0,1:T(8,128)(2,1)S(1)}, bf16[512,8,128]{2,0,1:T(8,128)(2,1)S(1)}, u32[]{:S(2)}, u32[]{:S(2)}) %collective-permute-start.1) | collective-permute-done | bytes 1048608 | tf_op jit(solution)/shard_map/ppermute | solution.py:63
  187.5 6.0 %collective-permute-done.8 = bf16[512,8,128]{2,0,1:T(8,128)(2,1)S(1)} collective-permute-done((bf16[512,8,128]{2,0,1:T(8,128)(2,1)S(1)}, bf16[512,8,128]{2,0,1:T(8,128)(2,1)S(1)}, u32[]{:S(2)}, u32[]{:S(2)}) %collective-permute-start.8) | collective-permute-done | bytes 1048608 | tf_op jit(solution)/shard_map/ppermute | solution.py:63
  221.2 6.0 %collective-permute-done.24 = bf16[512,8,128]{2,0,1:T(8,128)(2,1)S(1)} collective-permute-done((bf16[512,8,128]{2,0,1:T(8,128)(2,1)S(1)}, bf16[512,8,128]{2,0,1:T(8,128)(2,1)S(1)}, u32[]{:S(2)}, u32[]{:S(2)}) %collective-permute-start.24) | collective-permute-done | bytes 1048608 | tf_op jit(solution)/shard_map/ppermute | solution.py:64
  232.4 6.0 %collective-permute-done.10 = bf16[512,8,128]{2,0,1:T(8,128)(2,1)S(1)} collective-permute-done((bf16[512,8,128]{2,0,1:T(8,128)(2,1)S(1)}, bf16[512,8,128]{2,0,1:T(8,128)(2,1)S(1)}, u32[]{:S(2)}, u32[]{:S(2)}) %collective-permute-start.10) | collective-permute-done | bytes 1048608 | tf_op jit(solution)/shard_map/ppermute | solution.py:63
  288.6 6.0 %collective-permute-done.27 = bf16[512,8,128]{2,0,1:T(8,128)(2,1)S(1)} collective-permute-done((bf16[512,8,128]{2,0,1:T(8,128)(2,1)S(1)}, bf16[512,8,128]{2,0,1:T(8,128)(2,1)S(1)}, u32[]{:S(2)}, u32[]{:S(2)}) %collective-permute-start.27) | collective-permute-done | bytes 1048608 | tf_op jit(solution)/shard_map/ppermute | solution.py:64
  311.1 6.0 %collective-permute-done.28 = bf16[512,8,128]{2,0,1:T(8,128)(2,1)} collective-permute-done((bf16[512,8,128]{2,0,1:T(8,128)(2,1)S(1)}, bf16[512,8,128]{2,0,1:T(8,128)(2,1)}, u32[]{:S(2)}, u32[]{:S(2)}) %collective-permute-start.28) | collective-permute-done | bytes 1048608 | tf_op jit(solution)/shard_map/ppermute | solution.py:64
  323.1 7.8 %fusion.603 = f32[8,3,256,128]{3,2,1,0:T(8,128)S(1)} fusion(f32[8,3,256,512]{3,2,1,0:T(8,128)} %copy-done.1, f32[8,3,256]{2,1,0:T(4,128)S(1)} %get-tuple-element.1245, pred[256,512]{1,0:T(8,128)(4,1)S(1)} %iota_compare_fusion, bf16[512,8,128,1]{2,1,0,3:T(8,128)(2,1)} %bitcast.520), kind=kOutput, calls=%fused_computation.695 | convolution fusion | flops 817889280 | bytes 16932864 | tf_op jit(solution)/shard_map/kgqs,skd->kgqd/dot_general | solution.py:12
  330.9 9.4 %conditional.15 = (f32[8,3,256]{2,1,0:T(4,128)S(1)}, f32[8,3,256]{2,1,0:T(4,128)S(1)}, f32[8,3,256,128]{3,2,1,0:T(8,128)S(1)}, f32[8,3,256]{2,1,0:T(4,128)S(1)},...) conditional(s32[]{:T(128)} %convert_element_type.207, (bf16[8,3,256,128]{3,2,1,0:T(8,128)(2,1)S(1)}, ...), branch_computations={%region_4.7_spmd, %region_7.12_spmd} | conditional | flops 1638948864 | bytes 56541288 | solution.py:65
  340.3 10.7 %conditional.16 = (f32[8,3,256]{2,1,0:T(4,128)S(1)}, f32[8,3,256]{2,1,0:T(4,128)S(1)}, f32[8,3,256,128]{3,2,1,0:T(8,128)S(1)}, f32[8,3,256]{2,1,0:T(4,128)S(1)},...) conditional(s32[]{:T(128)} %convert_element_type.206, (bf16[8,3,256,128]{3,2,1,0:T(8,128)(2,1)S(1)}, ...), branch_computations={%region_12.15_spmd, %region_15.20_spmd} | conditional | flops 1638948864 | bytes 64929952 | solution.py:65
  351.0 10.7 %conditional.17 = (f32[8,3,256]{2,1,0:T(4,128)S(1)}, f32[8,3,256]{2,1,0:T(4,128)S(1)}, f32[8,3,256,128]{3,2,1,0:T(8,128)S(1)}, f32[8,3,256]{2,1,0:T(4,128)S(1)},...) conditional(s32[]{:T(128)} %convert_element_type.205, (bf16[8,3,256,128]{3,2,1,0:T(8,128)(2,1)S(1)}, ...), branch_computations={%region_20.23_spmd, %region_23.28_spmd} | conditional | flops 1638948864 | bytes 64929952 | solution.py:65
  361.8 10.8 %conditional.18 = (f32[8,3,256]{2,1,0:T(4,128)S(1)}, f32[8,3,256]{2,1,0:T(4,128)S(1)}, f32[8,3,256,128]{3,2,1,0:T(8,128)S(1)}, f32[8,3,256]{2,1,0:T(4,128)S(1)},...) conditional(s32[]{:T(128)} %convert_element_type.204, (bf16[8,3,256,128]{3,2,1,0:T(8,128)(2,1)S(1)}, ...), branch_computations={%region_28.31_spmd, %region_31.36_spmd} | conditional | flops 1638948864 | bytes 64929952 | solution.py:65
  372.6 11.0 %conditional.19 = (f32[8,3,256]{2,1,0:T(4,128)S(1)}, f32[8,3,256]{2,1,0:T(4,128)S(1)}, f32[8,3,256,128]{3,2,1,0:T(8,128)S(1)}, f32[8,3,256]{2,1,0:T(4,128)S(1)},...) conditional(s32[]{:T(128)} %convert_element_type.203, (bf16[8,3,256,128]{3,2,1,0:T(8,128)(2,1)S(1)}, ...), branch_computations={%region_36.39_spmd, %region_39.44_spmd} | conditional | flops 1638948864 | bytes 64929952 | solution.py:65
  383.6 10.7 %conditional.20 = (f32[8,3,256]{2,1,0:T(4,128)S(1)}, f32[8,3,256]{2,1,0:T(4,128)S(1)}, f32[8,3,256,128]{3,2,1,0:T(8,128)S(1)}, f32[8,3,256]{2,1,0:T(4,128)S(1)},...) conditional(s32[]{:T(128)} %convert_element_type.202, (bf16[8,3,256,128]{3,2,1,0:T(8,128)(2,1)S(1)}, ...), branch_computations={%region_44.47_spmd, %region_47.52_spmd} | conditional | flops 1638948864 | bytes 64929952 | solution.py:65
  394.3 10.7 %conditional.21 = (f32[8,3,256]{2,1,0:T(4,128)S(1)}, f32[8,3,256]{2,1,0:T(4,128)S(1)}, f32[8,3,256,128]{3,2,1,0:T(8,128)S(1)}, f32[8,3,256]{2,1,0:T(4,128)S(1)},...) conditional(s32[]{:T(128)} %convert_element_type.201, (bf16[8,3,256,128]{3,2,1,0:T(8,128)(2,1)S(1)}, ...), branch_computations={%region_52.55_spmd, %region_55.60_spmd} | conditional | flops 1638948864 | bytes 64929952 | solution.py:65
  405.1 10.8 %conditional.22 = (f32[8,3,256]{2,1,0:T(4,128)S(1)}, f32[8,3,256]{2,1,0:T(4,128)S(1)}, f32[8,3,256,128]{3,2,1,0:T(8,128)S(1)}, f32[8,3,256]{2,1,0:T(4,128)S(1)},...) conditional(s32[]{:T(128)} %convert_element_type.200, (bf16[8,3,256,128]{3,2,1,0:T(8,128)(2,1)S(1)}, ...), branch_computations={%region_60.63_spmd, %region_63.68_spmd} | conditional | flops 1638948864 | bytes 64929952 | solution.py:65
  415.9 11.0 %conditional.23 = (f32[8,3,256]{2,1,0:T(4,128)S(1)}, f32[8,3,256]{2,1,0:T(4,128)S(1)}, f32[8,3,256,128]{3,2,1,0:T(8,128)S(1)}, f32[8,3,256]{2,1,0:T(4,128)S(1)},...) conditional(s32[]{:T(128)} %convert_element_type.199, (bf16[8,3,256,128]{3,2,1,0:T(8,128)(2,1)S(1)}, ...), branch_computations={%region_68.71_spmd, %region_71.76_spmd} | conditional | flops 1638948864 | bytes 64929952 | solution.py:65
  426.9 10.7 %conditional.24 = (f32[8,3,256]{2,1,0:T(4,128)S(1)}, f32[8,3,256]{2,1,0:T(4,128)S(1)}, f32[8,3,256,128]{3,2,1,0:T(8,128)S(1)}, f32[8,3,256]{2,1,0:T(4,128)S(1)},...) conditional(s32[]{:T(128)} %convert_element_type.198, (bf16[8,3,256,128]{3,2,1,0:T(8,128)(2,1)S(1)}, ...), branch_computations={%region_76.79_spmd, %region_79.84_spmd} | conditional | flops 1638948864 | bytes 64929952 | solution.py:65
  437.6 10.7 %conditional.25 = (f32[8,3,256]{2,1,0:T(4,128)S(1)}, f32[8,3,256]{2,1,0:T(4,128)S(1)}, f32[8,3,256,128]{3,2,1,0:T(8,128)S(1)}, f32[8,3,256]{2,1,0:T(4,128)S(1)},...) conditional(s32[]{:T(128)} %convert_element_type.197, (bf16[8,3,256,128]{3,2,1,0:T(8,128)(2,1)S(1)}, ...), branch_computations={%region_84.87_spmd, %region_87.92_spmd} | conditional | flops 1638948864 | bytes 64929952 | solution.py:65
  448.3 10.8 %conditional.26 = (f32[8,3,256]{2,1,0:T(4,128)S(1)}, f32[8,3,256]{2,1,0:T(4,128)S(1)}, f32[8,3,256,128]{3,2,1,0:T(8,128)S(1)}, f32[8,3,256]{2,1,0:T(4,128)S(1)},...) conditional(s32[]{:T(128)} %convert_element_type.196, (bf16[8,3,256,128]{3,2,1,0:T(8,128)(2,1)S(1)}, ...), branch_computations={%region_92.95_spmd, %region_95.100_spmd} | conditional | flops 1638948864 | bytes 64929952 | solution.py:65
  459.1 13.9 %conditional.27 = (f32[8,3,256]{2,1,0:T(4,128)}, f32[8,3,256]{2,1,0:T(4,128)S(1)}, f32[8,3,256,128]{3,2,1,0:T(8,128)S(1)}, f32[8,3,256]{2,1,0:T(4,128)S(1)}, f32...) conditional(s32[]{:T(128)} %convert_element_type.195, (bf16[8,3,256,128]{3,2,1,0:T(8,128)(2,1)S(1)}, ...), branch_computations={%region_100.103_spmd, %region_103.108_spmd} | conditional | flops 1638948864 | bytes 64872608 | solution.py:65
  473.1 16.2 %conditional.28 = (f32[8,3,256]{2,1,0:T(4,128)}, f32[8,3,256]{2,1,0:T(4,128)S(1)}, f32[8,3,256,128]{3,2,1,0:T(8,128)S(1)}, f32[8,3,256]{2,1,0:T(4,128)S(1)}, f32...) conditional(s32[]{:T(128)} %convert_element_type.194, (bf16[8,3,256,128]{3,2,1,0:T(8,128)(2,1)S(1)}, ...), branch_computations={%region_108.111_spmd, %region_111.116_spmd} | conditional | flops 1638948864 | bytes 56508520 | solution.py:65
  489.3 15.8 %conditional.29 = (f32[8,3,256]{2,1,0:T(4,128)S(1)}, f32[8,3,256,128]{3,2,1,0:T(8,128)S(1)}, f32[8,3,256]{2,1,0:T(4,128)S(1)}, f32[8,3,256,128]{3,2,1,0:T(8,128)S(1)}) conditional(s32[]{:T(128)} %convert_element_type.193, (bf16[8,3,256,128]{3,2,1,0:T(8,128)(2,1)S(1)}, bf16[512,8,128]{2,0,1:T(8,128)(2,1)}, f32[8,3,256]{2,1,0:T(4,128)S(1)}, ...), branch_computations={%region_116.119_spmd, %region_119.124_spmd} | conditional | flops 1638948864 | bytes 56262688 | solution.py:65
  (383 shorter events, 444.7 us)
Async XLA Ops:
  13.7 22.5 %collective-permute-start.1 = (bf16[512,8,128]{2,0,1:T(8,128)(2,1)S(1)}, bf16[512,8,128]{2,0,1:T(8,128)(2,1)S(1)}, u32[]{:S(2)}, u32[]{:S(2)}) collective-permute-start(bf16[512,8,128]{2,0,1:T(8,128)(2,1)S(1)} %collective-permute-done), channel_id=1, source_target_pairs={{0,1},{1,2},{2,3},{3,4},{4,5},{5,6},{6,7},{7,8},{8,9},{9,10},{10,1... | collective-permute-start | bytes 3145736 | tf_op jit(solution)/shard_map/ppermute | solution.py:63
  25.0 22.5 %collective-permute-start.16 = (bf16[512,8,128]{2,0,1:T(8,128)(2,1)S(1)}, bf16[512,8,128]{2,0,1:T(8,128)(2,1)S(1)}, u32[]{:S(2)}, u32[]{:S(2)}) collective-permute-start(bf16[512,8,128]{2,0,1:T(8,128)(2,1)S(1)} %collective-permute-done.15), channel_id=1, source_target_pairs={{0,1},{1,2},{2,3},{3,4},{4,5},{5,6},{6,7},{7,8},{8,9},{9,10},{10,1... | collective-permute-start | bytes 3145736 | tf_op jit(solution)/shard_map/ppermute | solution.py:64
  36.2 22.5 %collective-permute-start.2 = (bf16[512,8,128]{2,0,1:T(8,128)(2,1)S(1)}, bf16[512,8,128]{2,0,1:T(8,128)(2,1)S(1)}, u32[]{:S(2)}, u32[]{:S(2)}) collective-permute-start(bf16[512,8,128]{2,0,1:T(8,128)(2,1)S(1)} %collective-permute-done.1), channel_id=1, source_target_pairs={{0,1},{1,2},{2,3},{3,4},{4,5},{5,6},{6,7},{7,8},{8,9},{9,10},{10,1... | collective-permute-start | bytes 3145736 | tf_op jit(solution)/shard_map/ppermute | solution.py:63
  47.4 22.5 %collective-permute-start.17 = (bf16[512,8,128]{2,0,1:T(8,128)(2,1)S(1)}, bf16[512,8,128]{2,0,1:T(8,128)(2,1)S(1)}, u32[]{:S(2)}, u32[]{:S(2)}) collective-permute-start(bf16[512,8,128]{2,0,1:T(8,128)(2,1)S(1)} %collective-permute-done.16), channel_id=1, source_target_pairs={{0,1},{1,2},{2,3},{3,4},{4,5},{5,6},{6,7},{7,8},{8,9},{9,10},{10,1... | collective-permute-start | bytes 3145736 | tf_op jit(solution)/shard_map/ppermute | solution.py:64
  58.7 22.5 %collective-permute-start.3 = (bf16[512,8,128]{2,0,1:T(8,128)(2,1)S(1)}, bf16[512,8,128]{2,0,1:T(8,128)(2,1)S(1)}, u32[]{:S(2)}, u32[]{:S(2)}) collective-permute-start(bf16[512,8,128]{2,0,1:T(8,128)(2,1)S(1)} %collective-permute-done.2), channel_id=1, source_target_pairs={{0,1},{1,2},{2,3},{3,4},{4,5},{5,6},{6,7},{7,8},{8,9},{9,10},{10,1... | collective-permute-start | bytes 3145736 | tf_op jit(solution)/shard_map/ppermute | solution.py:63
  69.9 22.5 %collective-permute-start.18 = (bf16[512,8,128]{2,0,1:T(8,128)(2,1)S(1)}, bf16[512,8,128]{2,0,1:T(8,128)(2,1)S(1)}, u32[]{:S(2)}, u32[]{:S(2)}) collective-permute-start(bf16[512,8,128]{2,0,1:T(8,128)(2,1)S(1)} %collective-permute-done.17), channel_id=1, source_target_pairs={{0,1},{1,2},{2,3},{3,4},{4,5},{5,6},{6,7},{7,8},{8,9},{9,10},{10,1... | collective-permute-start | bytes 3145736 | tf_op jit(solution)/shard_map/ppermute | solution.py:64
  81.2 22.5 %collective-permute-start.4 = (bf16[512,8,128]{2,0,1:T(8,128)(2,1)S(1)}, bf16[512,8,128]{2,0,1:T(8,128)(2,1)S(1)}, u32[]{:S(2)}, u32[]{:S(2)}) collective-permute-start(bf16[512,8,128]{2,0,1:T(8,128)(2,1)S(1)} %collective-permute-done.3), channel_id=1, source_target_pairs={{0,1},{1,2},{2,3},{3,4},{4,5},{5,6},{6,7},{7,8},{8,9},{9,10},{10,1... | collective-permute-start | bytes 3145736 | tf_op jit(solution)/shard_map/ppermute | solution.py:63
  92.4 22.5 %collective-permute-start.19 = (bf16[512,8,128]{2,0,1:T(8,128)(2,1)S(1)}, bf16[512,8,128]{2,0,1:T(8,128)(2,1)S(1)}, u32[]{:S(2)}, u32[]{:S(2)}) collective-permute-start(bf16[512,8,128]{2,0,1:T(8,128)(2,1)S(1)} %collective-permute-done.18), channel_id=1, source_target_pairs={{0,1},{1,2},{2,3},{3,4},{4,5},{5,6},{6,7},{7,8},{8,9},{9,10},{10,1... | collective-permute-start | bytes 3145736 | tf_op jit(solution)/shard_map/ppermute | solution.py:64
  103.6 22.5 %collective-permute-start.5 = (bf16[512,8,128]{2,0,1:T(8,128)(2,1)S(1)}, bf16[512,8,128]{2,0,1:T(8,128)(2,1)S(1)}, u32[]{:S(2)}, u32[]{:S(2)}) collective-permute-start(bf16[512,8,128]{2,0,1:T(8,128)(2,1)S(1)} %collective-permute-done.4), channel_id=1, source_target_pairs={{0,1},{1,2},{2,3},{3,4},{4,5},{5,6},{6,7},{7,8},{8,9},{9,10},{10,1... | collective-permute-start | bytes 3145736 | tf_op jit(solution)/shard_map/ppermute | solution.py:63
  114.9 22.5 %collective-permute-start.20 = (bf16[512,8,128]{2,0,1:T(8,128)(2,1)S(1)}, bf16[512,8,128]{2,0,1:T(8,128)(2,1)S(1)}, u32[]{:S(2)}, u32[]{:S(2)}) collective-permute-start(bf16[512,8,128]{2,0,1:T(8,128)(2,1)S(1)} %collective-permute-done.19), channel_id=1, source_target_pairs={{0,1},{1,2},{2,3},{3,4},{4,5},{5,6},{6,7},{7,8},{8,9},{9,10},{10,1... | collective-permute-start | bytes 3145736 | tf_op jit(solution)/shard_map/ppermute | solution.py:64
  126.1 22.5 %collective-permute-start.6 = (bf16[512,8,128]{2,0,1:T(8,128)(2,1)S(1)}, bf16[512,8,128]{2,0,1:T(8,128)(2,1)S(1)}, u32[]{:S(2)}, u32[]{:S(2)}) collective-permute-start(bf16[512,8,128]{2,0,1:T(8,128)(2,1)S(1)} %collective-permute-done.5), channel_id=1, source_target_pairs={{0,1},{1,2},{2,3},{3,4},{4,5},{5,6},{6,7},{7,8},{8,9},{9,10},{10,1... | collective-permute-start | bytes 3145736 | tf_op jit(solution)/shard_map/ppermute | solution.py:63
  137.3 22.5 %collective-permute-start.21 = (bf16[512,8,128]{2,0,1:T(8,128)(2,1)S(1)}, bf16[512,8,128]{2,0,1:T(8,128)(2,1)S(1)}, u32[]{:S(2)}, u32[]{:S(2)}) collective-permute-start(bf16[512,8,128]{2,0,1:T(8,128)(2,1)S(1)} %collective-permute-done.20), channel_id=1, source_target_pairs={{0,1},{1,2},{2,3},{3,4},{4,5},{5,6},{6,7},{7,8},{8,9},{9,10},{10,1... | collective-permute-start | bytes 3145736 | tf_op jit(solution)/shard_map/ppermute | solution.py:64
  148.6 22.5 %collective-permute-start.7 = (bf16[512,8,128]{2,0,1:T(8,128)(2,1)S(1)}, bf16[512,8,128]{2,0,1:T(8,128)(2,1)S(1)}, u32[]{:S(2)}, u32[]{:S(2)}) collective-permute-start(bf16[512,8,128]{2,0,1:T(8,128)(2,1)S(1)} %collective-permute-done.6), channel_id=1, source_target_pairs={{0,1},{1,2},{2,3},{3,4},{4,5},{5,6},{6,7},{7,8},{8,9},{9,10},{10,1... | collective-permute-start | bytes 3145736 | tf_op jit(solution)/shard_map/ppermute | solution.py:63
  159.8 22.5 %collective-permute-start.22 = (bf16[512,8,128]{2,0,1:T(8,128)(2,1)S(1)}, bf16[512,8,128]{2,0,1:T(8,128)(2,1)S(1)}, u32[]{:S(2)}, u32[]{:S(2)}) collective-permute-start(bf16[512,8,128]{2,0,1:T(8,128)(2,1)S(1)} %collective-permute-done.21), channel_id=1, source_target_pairs={{0,1},{1,2},{2,3},{3,4},{4,5},{5,6},{6,7},{7,8},{8,9},{9,10},{10,1... | collective-permute-start | bytes 3145736 | tf_op jit(solution)/shard_map/ppermute | solution.py:64
  171.0 22.5 %collective-permute-start.8 = (bf16[512,8,128]{2,0,1:T(8,128)(2,1)S(1)}, bf16[512,8,128]{2,0,1:T(8,128)(2,1)S(1)}, u32[]{:S(2)}, u32[]{:S(2)}) collective-permute-start(bf16[512,8,128]{2,0,1:T(8,128)(2,1)S(1)} %collective-permute-done.7), channel_id=1, source_target_pairs={{0,1},{1,2},{2,3},{3,4},{4,5},{5,6},{6,7},{7,8},{8,9},{9,10},{10,1... | collective-permute-start | bytes 3145736 | tf_op jit(solution)/shard_map/ppermute | solution.py:63
  182.3 22.5 %collective-permute-start.23 = (bf16[512,8,128]{2,0,1:T(8,128)(2,1)S(1)}, bf16[512,8,128]{2,0,1:T(8,128)(2,1)S(1)}, u32[]{:S(2)}, u32[]{:S(2)}) collective-permute-start(bf16[512,8,128]{2,0,1:T(8,128)(2,1)S(1)} %collective-permute-done.22), channel_id=1, source_target_pairs={{0,1},{1,2},{2,3},{3,4},{4,5},{5,6},{6,7},{7,8},{8,9},{9,10},{10,1... | collective-permute-start | bytes 3145736 | tf_op jit(solution)/shard_map/ppermute | solution.py:64
  193.5 22.5 %collective-permute-start.9 = (bf16[512,8,128]{2,0,1:T(8,128)(2,1)S(1)}, bf16[512,8,128]{2,0,1:T(8,128)(2,1)S(1)}, u32[]{:S(2)}, u32[]{:S(2)}) collective-permute-start(bf16[512,8,128]{2,0,1:T(8,128)(2,1)S(1)} %collective-permute-done.8), channel_id=1, source_target_pairs={{0,1},{1,2},{2,3},{3,4},{4,5},{5,6},{6,7},{7,8},{8,9},{9,10},{10,1... | collective-permute-start | bytes 3145736 | tf_op jit(solution)/shard_map/ppermute | solution.py:63
  204.7 22.5 %collective-permute-start.24 = (bf16[512,8,128]{2,0,1:T(8,128)(2,1)S(1)}, bf16[512,8,128]{2,0,1:T(8,128)(2,1)S(1)}, u32[]{:S(2)}, u32[]{:S(2)}) collective-permute-start(bf16[512,8,128]{2,0,1:T(8,128)(2,1)S(1)} %collective-permute-done.23), channel_id=1, source_target_pairs={{0,1},{1,2},{2,3},{3,4},{4,5},{5,6},{6,7},{7,8},{8,9},{9,10},{10,1... | collective-permute-start | bytes 3145736 | tf_op jit(solution)/shard_map/ppermute | solution.py:64
  216.0 22.5 %collective-permute-start.10 = (bf16[512,8,128]{2,0,1:T(8,128)(2,1)S(1)}, bf16[512,8,128]{2,0,1:T(8,128)(2,1)S(1)}, u32[]{:S(2)}, u32[]{:S(2)}) collective-permute-start(bf16[512,8,128]{2,0,1:T(8,128)(2,1)S(1)} %collective-permute-done.9), channel_id=1, source_target_pairs={{0,1},{1,2},{2,3},{3,4},{4,5},{5,6},{6,7},{7,8},{8,9},{9,10},{10,1... | collective-permute-start | bytes 3145736 | tf_op jit(solution)/shard_map/ppermute | solution.py:63
  227.2 22.5 %collective-permute-start.25 = (bf16[512,8,128]{2,0,1:T(8,128)(2,1)S(1)}, bf16[512,8,128]{2,0,1:T(8,128)(2,1)S(1)}, u32[]{:S(2)}, u32[]{:S(2)}) collective-permute-start(bf16[512,8,128]{2,0,1:T(8,128)(2,1)S(1)} %collective-permute-done.24), channel_id=1, source_target_pairs={{0,1},{1,2},{2,3},{3,4},{4,5},{5,6},{6,7},{7,8},{8,9},{9,10},{10,1... | collective-permute-start | bytes 3145736 | tf_op jit(solution)/shard_map/ppermute | solution.py:64
  272.2 22.5 %collective-permute-start.27 = (bf16[512,8,128]{2,0,1:T(8,128)(2,1)S(1)}, bf16[512,8,128]{2,0,1:T(8,128)(2,1)S(1)}, u32[]{:S(2)}, u32[]{:S(2)}) collective-permute-start(bf16[512,8,128]{2,0,1:T(8,128)(2,1)S(1)} %collective-permute-done.26), channel_id=1, source_target_pairs={{0,1},{1,2},{2,3},{3,4},{4,5},{5,6},{6,7},{7,8},{8,9},{9,10},{10,1... | collective-permute-start | bytes 3145736 | tf_op jit(solution)/shard_map/ppermute | solution.py:64
  294.6 22.5 %collective-permute-start.28 = (bf16[512,8,128]{2,0,1:T(8,128)(2,1)S(1)}, bf16[512,8,128]{2,0,1:T(8,128)(2,1)}, u32[]{:S(2)}, u32[]{:S(2)}) collective-permute-start(bf16[512,8,128]{2,0,1:T(8,128)(2,1)S(1)} %collective-permute-done.27), channel_id=1, source_target_pairs={{0,1},{1,2},{2,3},{3,4},{4,5},{5,6},{6,7},{7,8},{8,9},{9,10},{10,1... | collective-permute-start | bytes 3145736 | tf_op jit(solution)/shard_map/ppermute | solution.py:64
  305.9 183.4 %collective-permute-start.14 = (bf16[512,8,128]{2,0,1:T(8,128)(2,1)}, bf16[512,8,128]{2,0,1:T(8,128)(2,1)}, u32[]{:S(2)}, u32[]{:S(2)}) collective-permute-start(bf16[512,8,128]{2,0,1:T(8,128)(2,1)} %collective-permute-done.13), channel_id=1, source_target_pairs={{0,1},{1,2},{2,3},{3,4},{4,5},{5,6},{6,7},{7,8},{8,9},{9,10},{10,1... | collective-permute-start | bytes 3145736 | tf_op jit(solution)/shard_map/ppermute | solution.py:63
  317.1 172.2 %collective-permute-start.29 = (bf16[512,8,128]{2,0,1:T(8,128)(2,1)}, bf16[512,8,128]{2,0,1:T(8,128)(2,1)}, u32[]{:S(2)}, u32[]{:S(2)}) collective-permute-start(bf16[512,8,128]{2,0,1:T(8,128)(2,1)} %collective-permute-done.28), channel_id=1, source_target_pairs={{0,1},{1,2},{2,3},{3,4},{4,5},{5,6},{6,7},{7,8},{8,9},{9,10},{10,1... | collective-permute-start | bytes 3145736 | tf_op jit(solution)/shard_map/ppermute | solution.py:64
  (90 other events, 1452.3 us)
where the time goes:
time: 521 us; the launch traced here: 511 us
  waiting for transfers between devices  161 us (31%)
  starting transfers between devices  147 us (28%)
  matrix products  142 us (27%)
  other arithmetic  47.1 us (9%)
  local copies, waits for them, and re-layouts  8.54 us (2%)
  loops' own time  5.61 us (1%)
    ppermute x15, waiting for transfers between devices, local(): vb = lax.ppermute(vb, ('cy', 'cx'), perm)  84.5 us
    dot_general x30, matrix products, softmax_step(): jnp.einsum('kgqs,skd->kgqd', p.astype(jnp.bfloat16), vb, preferred_elemen...  79.7 us
    ppermute x15, waiting for transfers between devices, local(): kb = lax.ppermute(kb, ('cy', 'cx'), perm)  76.3 us
    ppermute x15, starting transfers between devices, local(): vb = lax.ppermute(vb, ('cy', 'cx'), perm)  73.4 us
    ppermute x15, starting transfers between devices, local(): kb = lax.ppermute(kb, ('cy', 'cx'), perm)  73.3 us
    dot_general x32, matrix products, scores(): jnp.einsum('kgqd,skd->kgqs', qx, kx, preferred_element_type=jnp.float32)  50.9 us
    reduce_sum x30, other arithmetic, softmax_step(): l = l * alpha + jnp.sum(p, axis=-1)  34.2 us
    dot_general x2, matrix products, softmax_first(): jnp.einsum('kgqs,skd->kgqd', p.astype(jnp.bfloat16), vb, preferred_elemen...  11.3 us
  transfers between devices with their start and end apart: 30, of which 28 were waited for; matrix products, arithmetic and copies ran while one was open for 34% of the time, Pallas kernels for 0%

commit v1 on v0

v1 whole, which is shorter than its diff:
```python
import functools
import math

import jax
import jax.numpy as jnp
from jax import lax
from jax.experimental import pallas as pl
from jax.experimental.pallas import tpu as pltpu
from jax.sharding import PartitionSpec as P


NX = 4
NZ = 4
SLOTS = 2
GQ = 3
NT = (((1,), (1,)), ((), ()))
MESH = pl.DeviceIdType.MESH
I = jnp.int32


def stage(c, qn, k_ref, v_ref, s_nxt, x_nxt, cur, base):
    rows, tq = k_ref.shape[0], qn.shape[0]
    bk = tq
    if cur is not None:
        s_cur, x_cur, m_ref, l_ref, a_ref = cur
        m0 = m_ref[...]
        m1 = jnp.maximum(m0, jnp.max(x_cur[...], axis=0, keepdims=True))
        al = jnp.exp2((m0 - m1) * c)
        m_ref[...] = m1
        lsum = l_ref[...] * al
    xm = o = None
    for b in range(rows // bk):
        r = slice(b * bk, (b + 1) * bk)
        s = lax.dot_general(k_ref[r, :], qn, NT, preferred_element_type=jnp.float32)
        if base is not None:
            kk = lax.broadcasted_iota(I, s.shape, 0) + b * bk
            qq = lax.broadcasted_iota(I, s.shape, 1) + base
            s = jnp.where(kk <= qq, s, -jnp.inf)
        s_nxt[r, :] = s
        y = jnp.max(s.reshape(bk // 8, 8, tq), axis=0)
        xm = y if xm is None else jnp.maximum(xm, y)
        if cur is not None:
            p = jnp.exp2((s_cur[r, :] - m1) * c)
            lsum = lsum + jnp.sum(p.reshape(bk // 8, 8, tq), axis=0)
            d = jnp.dot(v_ref[:, r], p.astype(jnp.bfloat16), preferred_element_type=jnp.float32)
            o = d if o is None else o + d
    x_nxt[...] = xm
    if cur is not None:
        l_ref[...] = lsum
        a_ref[...] = a_ref[...] * al + o


def unit(c, q_ref, k_ref, v_ref, m_ref, l_ref, a_ref, sa, sb, xa, xb, masked):
    tq = sa.shape[1]
    tiles = q_ref.shape[1] // tq
    n_all = GQ * tiles

    def base(n):
        return lax.rem(I(n), I(tiles)) * tq

    def qt(n):
        return q_ref[lax.div(I(n), I(tiles)), pl.ds(pl.multiple_of(base(n), tq), tq), :]

    def cur(n, s, x):
        return s, x, m_ref.at[n], l_ref.at[n], a_ref.at[n]

    stage(c, qt(0), k_ref, v_ref, sa, xa, None, base(0) if masked else None)

    @pl.loop(0, n_all // 2)
    def _(i):
        n = 2 * i
        stage(c, qt(n + 1), k_ref, v_ref, sb, xb, cur(n, sa, xa), base(n + 1) if masked else None)
        n2 = lax.rem(n + 2, I(n_all))
        stage(c, qt(n2), k_ref, v_ref, sa, xa, cur(n + 1, sb, xb), base(n2) if masked else None)


def kernel(c, q, k, v, o, qb, kb, vb, m, l, a, ost, sa, sb, xa, xb,
           xsend, xrecv, xloc, zrecv, dsend, usend, osend, orecv):
    z = lax.axis_index("cy")
    j = lax.axis_index("cx")
    pc = k.shape[1] // 2
    top = 2 * NZ - 1
    tiles = qb.shape[3] // pc

    def mod(x):
        return lax.rem(x + 2 * NX, I(NX))

    def chunk(part):
        return z if part == 0 else top - z

    def pos(part, jj):
        return jj if part == 0 else NX - 1 - jj

    def span(part, jj):
        return pl.ds(pl.multiple_of(pos(part, jj) * pc, pc), pc)

    barrier = pltpu.get_barrier_semaphore()
    for p in range(1, NX):
        pl.semaphore_signal(barrier, inc=1, device_id={"cx": mod(j + p)}, device_id_type=MESH)

    @pl.when(z > 0)
    def _():
        pl.semaphore_signal(barrier, inc=1, device_id={"cy": z - 1}, device_id_type=MESH)

    @pl.when(z < NZ - 1)
    def _():
        pl.semaphore_signal(barrier, inc=1, device_id={"cy": z + 1}, device_id_type=MESH)

    pl.semaphore_wait(barrier, NX - 1 + jnp.where(z > 0, 1, 0) + jnp.where(z < NZ - 1, 1, 0))

    def pair(g, kind, part, owner, dest):
        half = pl.ds(part * pc, pc)
        at = span(part, owner)
        if kind == 0:
            return k.at[SLOTS * dest + g, half, :], kb.at[g, chunk(part), at, :]
        if kind == 1:
            return v.at[SLOTS * dest + g, :, half], vb.at[g, chunk(part), :, at]
        return q.at[pl.ds(GQ * (SLOTS * dest + g), GQ), half, :], qb.at[g, part, :, at, :]

    def xcopy(g, kind, part, p, owner, dest):
        src, dst = pair(g, kind, part, owner, dest)
        return pltpu.make_async_remote_copy(
            src_ref=src, dst_ref=dst, send_sem=xsend.at[g, kind, part, p - 1], recv_sem=xrecv.at[g, kind, part, p - 1],
            device_id={"cx": dest}, device_id_type=MESH)

    def xlocal(g, kind, part):
        src, dst = pair(g, kind, part, j, j)
        return pltpu.make_async_copy(src, dst, xloc.at[g, kind, part])

    def xwait(g, kinds):
        for kind in kinds:
            for part in range(2):
                xlocal(g, kind, part).wait()
                for p in range(1, NX):
                    xcopy(g, kind, part, p, mod(j - p), j).wait_recv()

    for g in range(SLOTS):
        for kinds in ((0, 1), (2,)):
            for p in range(1, NX):
                for kind in kinds:
                    for part in range(2):
                        xcopy(g, kind, part, p, j, mod(j + p)).start()
            for kind in kinds:
                for part in range(2):
                    xlocal(g, kind, part).start()

    def zcopies(g, ch, dz, send):
        return [
            pltpu.make_async_remote_copy(
                src_ref=buf.at[g, ch], dst_ref=buf.at[g, ch], send_sem=send.at[g, ch, i], recv_sem=zrecv.at[g, ch, i],
                device_id={"cy": z + dz}, device_id_type=MESH)
            for i, buf in enumerate((kb, vb))
        ]

    def down(g, ch):
        @pl.when(z > 0)
        def _():
            for d in zcopies(g, ch, -1, dsend):
                d.start()

    def up(g, ch):
        @pl.when(z < NZ - 1)
        def _():
            for d in zcopies(g, ch, 1, usend):
                d.start()

    m[...] = jnp.full_like(m, -jnp.inf)
    l[...] = jnp.zeros_like(l)

    @pl.loop(0, SLOTS * 2)
    def _(i):
        a[lax.div(i, I(2)), lax.rem(i, I(2))] = jnp.zeros(a.shape[2:], a.dtype)

    def run(g, qc, ch, masked):
        unit(c, qb.at[g, qc], kb.at[g, ch], vb.at[g, ch], m.at[g, qc], l.at[g, qc], a.at[g, qc], sa, sb, xa, xb, masked)

    def ocopy(g, part, p, owner, dest):
        return pltpu.make_async_remote_copy(
            src_ref=ost.at[g, part, :, span(part, dest), :],
            dst_ref=o.at[pl.ds(GQ * (SLOTS * owner + g), GQ), pl.ds(part * pc, pc), :],
            send_sem=osend.at[g, part, p], recv_sem=orecv.at[g, part, p - 1],
            device_id={"cx": dest}, device_id_type=MESH)

    def olocal(g, part):
        return pltpu.make_async_copy(
            ost.at[g, part, :, span(part, j), :], o.at[pl.ds(GQ * (SLOTS * j + g), GQ), pl.ds(part * pc, pc), :],
            osend.at[g, part, 0])

    @pl.loop(0, NZ * SLOTS)
    def _(step):
        t = lax.div(step, I(SLOTS))
        g = lax.rem(step, I(SLOTS))
        below = (t > 0) & (z >= t)
        above = (t > 0) & (z + t < NZ)

        @pl.when(t == 0)
        def _():
            xwait(g, (0, 1))
            for ch in (z, top - z):
                down(g, ch)
            up(g, z)
            xwait(g, (2,))

            @pl.loop(0, 2)
            def _(qc):
                run(g, qc, jnp.where(qc == 0, z, top - z), True)

        nb = jnp.where(below, 2, 0)
        nu = jnp.where(t == 0, 1, nb + jnp.where(above, 2, 0))

        @pl.loop(0, nu)
        def _(u):
            is_below = u < nb
            s = z + t
            ch = jnp.where(t == 0, z, jnp.where(is_below, z - t, jnp.where(u == nb, s, top - s)))
            qc = jnp.where(is_below, u, 1)

            @pl.when(is_below & (u == 0))
            def _():
                for d in zcopies(g, ch, 1, usend):
                    d.wait_recv()
                up(g, ch)

            @pl.when((t > 0) & (u >= nb))
            def _():
                for d in zcopies(g, ch, -1, dsend):
                    d.wait_recv()
                down(g, ch)

            run(g, qc, ch, False)

        @pl.when(t == NZ - 1)
        def _():
            for part in range(2):
                @pl.loop(0, GQ * tiles)
                def _(n):
                    y = a[g, part, n] / jnp.sum(l[g, part, n], axis=0, keepdims=True)
                    at = pl.ds(pl.multiple_of(lax.rem(n, I(tiles)) * pc, pc), pc)
                    ost[g, part, lax.div(n, I(tiles)), at, :] = y.T.astype(ost.dtype)
            for part in range(2):
                for p in range(1, NX):
                    ocopy(g, part, p, j, mod(j + p)).start()
                olocal(g, part).start()

    for g in range(SLOTS):
        for part in range(2):
            olocal(g, part).wait()
            for p in range(1, NX):
                ocopy(g, part, p, mod(j - p), j).wait_recv()
                ocopy(g, part, p, j, mod(j + p)).wait_send()
                for kind in range(3):
                    xcopy(g, kind, part, p, j, mod(j + p)).wait_send()
        for s in range(NZ):
            @pl.when((z > 0) & (s >= z))
            def _():
                for ch in (s, top - s):
                    for d in zcopies(g, ch, -1, dsend):
                        d.wait_send()

            @pl.when((z < NZ - 1) & (s <= z))
            def _():
                for d in zcopies(g, s, 1, usend):
                    d.wait_send()


def solution(mesh):
    assert mesh.shape["cx"] == NX and mesh.shape["cy"] == NZ
    spec = P(("batch", "cy", "cx"), None, None)

    def local(q, k, v):
        t, h, d = q.shape
        pc = t // 2
        rows = NX * pc
        c = d ** -0.5 * math.log2(math.e)
        tiles = rows // pc
        f32, bf = jnp.float32, jnp.bfloat16
        dma = pltpu.SemaphoreType.DMA
        ot = pl.pallas_call(
            functools.partial(kernel, c),
            out_shape=jax.ShapeDtypeStruct((h, t, d), bf),
            in_specs=[pl.BlockSpec(memory_space=pl.ANY)] * 3,
            out_specs=pl.BlockSpec(memory_space=pl.ANY),
            scratch_shapes=[
                pltpu.VMEM((SLOTS, 2, GQ, rows, d), bf),
                pltpu.VMEM((SLOTS, 2 * NZ, rows, d), bf),
                pltpu.VMEM((SLOTS, 2 * NZ, d, rows), bf),
                pltpu.VMEM((SLOTS, 2, GQ * tiles, 1, pc), f32),
                pltpu.VMEM((SLOTS, 2, GQ * tiles, 8, pc), f32),
                pltpu.VMEM((SLOTS, 2, GQ * tiles, d, pc), f32),
                pltpu.VMEM((SLOTS, 2, GQ, rows, d), bf),
                pltpu.VMEM((rows, pc), f32),
                pltpu.VMEM((rows, pc), f32),
                pltpu.VMEM((8, pc), f32),
                pltpu.VMEM((8, pc), f32),
                dma((SLOTS, 3, 2, NX - 1)),
                dma((SLOTS, 3, 2, NX - 1)),
                dma((SLOTS, 3, 2)),
                dma((SLOTS, 2 * NZ, 2)),
                dma((SLOTS, 2 * NZ, 2)),
                dma((SLOTS, 2 * NZ, 2)),
                dma((SLOTS, 2, NX)),
                dma((SLOTS, 2, NX - 1)),
            ],
            compiler_params=pltpu.CompilerParams(
                collective_id=0, has_side_effects=True, vmem_limit_bytes=56 * 2**20),
        )(jnp.transpose(q, (1, 0, 2)), jnp.transpose(k, (1, 0, 2)), jnp.transpose(v, (1, 2, 0)))
        return jnp.transpose(ot, (1, 0, 2))

    return jax.shard_map(local, mesh=mesh, in_specs=(spec, spec, spec), out_specs=spec, check_vma=False)
```

time: 521 us -> 209 us (0.40)
  the two profiles are of different devices: /device:TPU:31 before, /device:TPU:0 now
where the time goes in v1:
time: 209 us; the launch traced here: 207 us
  Pallas kernels  194 us (93%)
  local copies, waits for them, and re-layouts  12.9 us (6%)
    pallas_call x1, Pallas kernels, local(): pl.pallas_call(functools.partial(kernel, c), out_shape=jax.ShapeDtypeStru...  194 us
    unnamed x5, local copies, waits for them, and re-layouts  7.29 us
    transpose x1, local copies, waits for them, and re-layouts, local(): return jnp.transpose(ot, (1, 0, 2))  5.58 us

profile of v1, /device:TPU:0, one launch (start us, length us, event | category | flops | bytes accessed | tf_op | source)
XLA Modules:
  0.0 207.2 jit_solution(14518122926389092627)
XLA Ops:
  0.0 0.0 copy-start
  0.0 2.5 %copy.11 = bf16[512,8,128]{2,0,1:T(8,128)(2,1)} copy(bf16[512,8,128]{2,1,0:T(8,128)(2,1)} %param.4) | data formatting | bytes 2097152 | tf_op args[1]
  2.5 2.4 %copy.6 = bf16[512,8,128]{0,2,1:T(8,128)(2,1)} copy(bf16[512,8,128]{2,1,0:T(8,128)(2,1)} %param.5) | data formatting | bytes 2097152 | tf_op args[2]
  4.9 0.0 copy-done
  4.9 2.4 %copy.10 = bf16[512,24,128]{2,0,1:T(8,128)(2,1)} copy(bf16[512,24,128]{2,1,0:T(8,128)(2,1)S(1)} %copy-done) | data formatting | bytes 6291456 | tf_op args[0]
  7.3 194.3 %shard_map.37 = bf16[24,512,128]{2,1,0:T(8,128)(2,1)} custom-call(bf16[24,512,128]{2,1,0:T(8,128)(2,1)} %bitcast.9, bf16[8,512,128]{2,1,0:T(8,128)(2,1)} %bitcast.10, bf16[8,128,512]{2,1,0:T(8,128)(2,1)} %bitcast.11), custom_call_target="tpu_custom_call" | custom-call | tf_op jit(solution)/shard_map/pallas_call | solution.py:278
  201.6 5.6 %copy.7 = bf16[512,24,128]{2,1,0:T(8,128)(2,1)} copy(bf16[512,24,128]{2,0,1:T(8,128)(2,1)} %bitcast.8) | data formatting | bytes 6291456 | tf_op jit(solution)/shard_map/transpose | solution.py:307
Async XLA Ops:
  0.0 4.9 %copy-start = (bf16[512,24,128]{2,1,0:T(8,128)(2,1)S(1)}, bf16[512,24,128]{2,1,0:T(8,128)(2,1)}, u32[]{:S(2)}) copy-start(bf16[512,24,128]{2,1,0:T(8,128)(2,1)} %param.3) | copy-start | bytes 9437188

commit v2 on v1

v2 whole, which is shorter than its diff:
```python
import functools
import math

import jax
import jax.numpy as jnp
from jax import lax
from jax.experimental import pallas as pl
from jax.experimental.pallas import tpu as pltpu
from jax.sharding import PartitionSpec as P


NX = 4
NZ = 4
SLOTS = 2
GQ = 3
NB = 4
NT = (((1,), (1,)), ((), ()))
MESH = pl.DeviceIdType.MESH
I = jnp.int32


def stage(c, nxt, cur):
    qn, kn_ref, s_nxt, x_nxt, base = nxt
    rows, tq = kn_ref.shape[0], qn.shape[0]
    bk = rows // NB
    if cur is not None:
        s_cur, x_cur, v_ref, m_ref, l_ref, a_ref = cur
        m0 = m_ref[...]
        m1 = jnp.maximum(m0, jnp.max(x_cur[...], axis=0, keepdims=True))
        al = jnp.exp2((m0 - m1) * c)
        m_ref[...] = m1
        lsum = l_ref[...] * al
    xm = o = None
    for b in range(rows // bk):
        r = slice(b * bk, (b + 1) * bk)
        s = lax.dot_general(kn_ref[r, :], qn, NT, preferred_element_type=jnp.float32)
        if base is not None:
            kk = lax.broadcasted_iota(I, s.shape, 0) + b * bk
            qq = lax.broadcasted_iota(I, s.shape, 1) + base
            s = jnp.where(kk <= qq, s, -jnp.inf)
        s_nxt[r, :] = s
        y = jnp.max(s.reshape(bk // 8, 8, tq), axis=0)
        xm = y if xm is None else jnp.maximum(xm, y)
        if cur is not None:
            p = jnp.exp2((s_cur[r, :] - m1) * c)
            lsum = lsum + jnp.sum(p.reshape(bk // 8, 8, tq), axis=0)
            d = jnp.dot(v_ref[:, r], p.astype(jnp.bfloat16), preferred_element_type=jnp.float32)
            o = d if o is None else o + d
    x_nxt[...] = xm
    if cur is not None:
        l_ref[...] = lsum
        a_ref[...] = a_ref[...] * al + o


SHIFT = 4
TOP = 2 * NZ - 1
START, EXTRA, BELOW, ABOVE = 1, 2, 3, 4


def units(z):
    out = []
    for g in range(SLOTS):
        has_high = not (z == 0 and g == 1)
        out.append((2 * g, g, z, 1, START))
        if has_high:
            out.append((2 * g + 1, g, TOP - z, 1, 0))
            out.append((2 * g + 1, g, z, 0, 0))
    if z == 1:
        out += [(SHIFT, 1, TOP, 1, EXTRA), (SHIFT, 1, z, 0, 0), (SHIFT, 1, TOP - z, 0, 0)]
    for t in range(1, NZ):
        for g in range(SLOTS):
            extra = z == 1 and g == 1
            if z >= t:
                s = z - t
                out.append((2 * g, g, s, 0, BELOW))
                if extra:
                    out.append((SHIFT, g, s, 0, 0))
                out.append((2 * g + 1, g, s, 0, 0))
            if z + t < NZ and not (z == 0 and g == 1):
                for ch in (z + t, TOP - z - t):
                    if extra:
                        out.append((SHIFT, g, ch, 0, ABOVE))
                    out.append((2 * g + 1, g, ch, 0, 0 if extra else ABOVE))
    last = {u[0]: i for i, u in enumerate(out)}
    return [u + (int(last[u[0]] == i),) for i, u in enumerate(out)]


RADIX = (5, 2, 8, 2, 5, 2)


def pack(u):
    x = 0
    for r, f in zip(RADIX, u):
        x = x * r + f
    return x


def unpack(x):
    out = []
    for r in RADIX[::-1]:
        out.append(lax.rem(x, I(r)))
        x = lax.div(x, I(r))
    return out[::-1]


def kernel(c, q, k, v, o, qb, kb, vb, m, l, a, ost, sa, sb, xa, xb,
           xsend, xrecv, xloc, zrecv, dsend, usend, osend, orecv):
    z = lax.axis_index("cy")
    j = lax.axis_index("cx")
    pc = k.shape[1] // 2
    tq = sa.shape[1]
    tiles = qb.shape[2] // tq
    n_all = GQ * tiles

    def mod(x):
        return lax.rem(x + 2 * NX, I(NX))

    def chunk(part):
        return z if part == 0 else TOP - z

    def pos(part, jj):
        return jj if part == 0 else NX - 1 - jj

    def span(part, jj):
        return pl.ds(pl.multiple_of(pos(part, jj) * pc, pc), pc)

    barrier = pltpu.get_barrier_semaphore()
    for p in range(1, NX):
        pl.semaphore_signal(barrier, inc=1, device_id={"cx": mod(j + p)}, device_id_type=MESH)

    @pl.when(z > 0)
    def _():
        pl.semaphore_signal(barrier, inc=1, device_id={"cy": z - 1}, device_id_type=MESH)

    @pl.when(z < NZ - 1)
    def _():
        pl.semaphore_signal(barrier, inc=1, device_id={"cy": z + 1}, device_id_type=MESH)

    @pl.when(z < 2)
    def _():
        for p in range(1, NX):
            pl.semaphore_signal(barrier, inc=1, device_id={"cy": 1 - z, "cx": mod(j + p)}, device_id_type=MESH)

    def by_z(values):
        x = I(values[-1])
        for zz in range(NZ - 1):
            x = jnp.where(z == zz, I(values[zz]), x)
        return x

    lists = [[pack(u) for u in units(zz)] for zz in range(NZ)]
    count = by_z([len(x) for x in lists])
    codes = [by_z([x[min(i, len(x) - 1)] for x in lists]) for i in range(max(map(len, lists)))]

    def fields(u):
        x = codes[-1]
        for i, code in enumerate(codes[:-1]):
            x = jnp.where(u == i, code, x)
        return unpack(x)

    pl.semaphore_wait(
        barrier, NX - 1 + jnp.where(z > 0, 1, 0) + jnp.where(z < NZ - 1, 1, 0) + jnp.where(z < 2, NX - 1, 0))

    def pair(g, kind, part, e, owner, dest):
        half = pl.ds(part * pc, pc)
        at = span(part, owner)
        ch = I(TOP) if e == 2 else chunk(part)
        if kind == 0:
            return k.at[SLOTS * dest + g, half, :], kb.at[g, ch, at, :]
        if kind == 1:
            return v.at[SLOTS * dest + g, :, half], vb.at[g, ch, :, at]
        qs = SHIFT if e == 2 else 2 * g + part
        return q.at[pl.ds(GQ * (SLOTS * dest + g), GQ), half, :], qb.at[qs, :, at, :]

    def xcopy(g, kind, part, p, owner, dest, shifted=False):
        e = 2 if shifted else part
        src, dst = pair(g, kind, part, e, owner, dest)
        return pltpu.make_async_remote_copy(
            src_ref=src, dst_ref=dst, send_sem=xsend.at[g, kind, part, p], recv_sem=xrecv.at[g, kind, e, p],
            device_id={"cy": I(1) if shifted else z, "cx": dest}, device_id_type=MESH)

    def xlocal(g, kind, part):
        src, dst = pair(g, kind, part, part, j, j)
        return pltpu.make_async_copy(src, dst, xloc.at[g, kind, part])

    def xpart(g, part, fn, moved):
        if g == 1 and part == 1:
            pl.when(z == 0)(moved)
            pl.when(z > 0)(fn)
        else:
            fn()

    for g in range(SLOTS):
        for kinds in ((0, 1), (2,)):
            for part in range(2):
                def keep():
                    for p in range(1, NX):
                        for kind in kinds:
                            xcopy(g, kind, part, p, j, mod(j + p)).start()
                    for kind in kinds:
                        xlocal(g, kind, part).start()

                def give():
                    for p in range(NX):
                        for kind in kinds:
                            xcopy(g, kind, part, p, j, mod(j + p), True).start()

                xpart(g, part, keep, give)

    def xwait(g, kinds):
        for part in range(2):
            def keep():
                for kind in kinds:
                    xlocal(g, kind, part).wait()
                    for p in range(1, NX):
                        xcopy(g, kind, part, p, mod(j - p), j).wait_recv()

            xpart(g, part, keep, lambda: None)

    def zcopies(g, ch, dz, send):
        return [
            pltpu.make_async_remote_copy(
                src_ref=buf.at[g, ch], dst_ref=buf.at[g, ch], send_sem=send.at[g, ch, i], recv_sem=zrecv.at[g, ch, i],
                device_id={"cy": z + dz}, device_id_type=MESH)
            for i, buf in enumerate((kb, vb))
        ]

    def goes_down(g):
        return z > jnp.where(g == 1, 1, 0)

    def down(g, ch):
        @pl.when(goes_down(g))
        def _():
            for d in zcopies(g, ch, -1, dsend):
                d.start()

    def up(g, ch):
        @pl.when(z < NZ - 1)
        def _():
            for d in zcopies(g, ch, 1, usend):
                d.start()

    m[...] = jnp.full_like(m, -jnp.inf)
    l[...] = jnp.zeros_like(l)

    @pl.loop(0, 5)
    def _(i):
        a[i] = jnp.zeros(a.shape[1:], a.dtype)

    def before(f):
        _, g, ch, _, act, _ = f
        for gg in range(SLOTS):
            @pl.when((act == START) & (g == gg))
            def _():
                xwait(gg, (0, 1))
                down(I(gg), z)
                up(I(gg), z)
                pl.when(z > 0)(lambda: down(I(gg), TOP - z))
                xwait(gg, (2,))

        @pl.when(act == EXTRA)
        def _():
            for kind in range(3):
                for p in range(NX):
                    xcopy(1, kind, 1, p, mod(j - p), j, True).wait_recv()

        @pl.when(act == BELOW)
        def _():
            for d in zcopies(g, ch, 1, usend):
                d.wait_recv()
            up(g, ch)

        @pl.when(act == ABOVE)
        def _():
            for d in zcopies(g, ch, -1, dsend):
                d.wait_recv()
            down(g, ch)

    def opiece(g, part, p, owner, dest, heads, hd, shifted):
        qs = SHIFT if shifted else 2 * g + part
        return dict(
            src_ref=ost.at[qs, pl.ds(hd, heads), span(part, dest), :],
            dst_ref=o.at[pl.ds(GQ * (SLOTS * owner + g) + hd, heads), pl.ds(part * pc, pc), :])

    def oremote(g, part, p, owner, dest, heads=GQ, hd=0, shifted=False):
        return pltpu.make_async_remote_copy(
            **opiece(g, part, p, owner, dest, heads, hd, shifted),
            send_sem=osend.at[SHIFT if shifted else 2 * g + part, p], recv_sem=orecv.at[2 * g + part, p],
            device_id={"cy": I(0) if shifted else z, "cx": dest}, device_id_type=MESH)

    def olocal(g, part, heads=GQ, hd=0):
        r = opiece(g, part, 0, j, j, heads, hd, False)
        return pltpu.make_async_copy(r["src_ref"], r["dst_ref"], osend.at[2 * g + part, 0])

    def finish(qs, n):
        y = a[qs, n] / jnp.sum(l[qs, n], axis=0, keepdims=True)
        at = pl.ds(pl.multiple_of(lax.rem(n, I(tiles)) * tq, tq), tq)
        ost[qs, lax.div(n, I(tiles)), at, :] = y.astype(ost.dtype).T

    def give_back(qs, n):
        hd = lax.div(n, I(tiles))
        for case in range(5):
            @pl.when(qs == case)
            def _():
                shifted = case == SHIFT
                g, part = (1, 1) if shifted else (case // 2, case % 2)
                for e in range(tq // pc):
                    at = lax.rem(n, I(tiles)) * (tq // pc) + e
                    dest = pos(part, at)
                    p = mod(dest - j)
                    if shifted:
                        oremote(g, part, p, j, dest, 1, hd, True).start()
                    else:
                        pl.when(p == 0)(lambda: olocal(g, part, 1, hd).start())
                        pl.when(p > 0)(lambda: oremote(g, part, p, j, dest, 1, hd).start())

    def after(f, w, n):
        pl.when(f[5] == 1)(lambda: finish(f[0], n))
        pl.when(w[5] == 1)(lambda: give_back(w[0], lax.rem(n + n_all - 1, I(n_all))))

    def nxt(f, n, s, x, masked):
        base = lax.rem(I(n), I(tiles)) * tq
        at = pl.ds(pl.multiple_of(base, tq), tq)
        return qb[f[0], lax.div(I(n), I(tiles)), at, :], kb.at[f[1], f[2]], s, x, base if masked else None

    def step(fn, nn, s_n, x_n, f, n, s_c, x_c):
        qs = f[0]
        for masked in (False, True):
            @pl.when(fn[3] == int(masked))
            def _():
                stage(c, nxt(fn, nn, s_n, x_n, masked),
                      (s_c, x_c, vb.at[f[1], f[2]], m.at[qs, n], l.at[qs, n], a.at[qs, n]))

    first = fields(I(0))
    before(first)
    stage(c, nxt(first, 0, sa, xa, True), None)

    @pl.loop(0, count)
    def _(u):
        f = fields(u)
        fn = fields(jnp.minimum(u + 1, count - 1))
        w = fields(jnp.maximum(u - 1, 0))
        w[5] = jnp.where(u > 0, w[5], 0)

        @pl.loop(0, n_all // 2)
        def _(i):
            n = 2 * i
            step(f, n + 1, sb, xb, f, n, sa, xa)
            after(f, [jnp.where(i == 0, p, q) for p, q in zip(w, f)], n)
            wrap = i == n_all // 2 - 1
            pl.when(wrap & (u + 1 < count))(lambda: before(fn))
            step([jnp.where(wrap, p, q) for p, q in zip(fn, f)], jnp.where(wrap, 0, n + 2), sa, xa, f, n + 1, sb, xb)
            after(f, f, n + 1)

    for g in range(SLOTS):
        for part in range(2):
            def keep():
                for p in range(1, NX):
                    for kind in range(3):
                        xcopy(g, kind, part, p, j, mod(j + p)).wait_send()

            def give():
                for p in range(NX):
                    for kind in range(3):
                        xcopy(g, kind, part, p, j, mod(j + p), True).wait_send()

            xpart(g, part, keep, give)
    give_back(fields(count - 1)[0], I(n_all - 1))
    for g in range(SLOTS):
        for s in range(NZ):
            @pl.when(goes_down(g) & (s >= z))
            def _():
                for ch in (s, TOP - s):
                    for d in zcopies(g, ch, -1, dsend):
                        d.wait_send()

            @pl.when((z < NZ - 1) & (s <= z))
            def _():
                for d in zcopies(g, s, 1, usend):
                    d.wait_send()
        for part in range(2):
            def keep():
                olocal(g, part).wait()
                for p in range(1, NX):
                    oremote(g, part, p, j, mod(j + p)).wait_send()
                    oremote(g, part, p, mod(j - p), j).wait_recv()

            def give():
                for p in range(NX):
                    oremote(g, part, p, mod(j - p), j).wait_recv()

            xpart(g, part, keep, give)

    @pl.when(z == 1)
    def _():
        for p in range(NX):
            oremote(1, 1, p, j, mod(j + p), shifted=True).wait_send()


def solution(mesh):
    assert mesh.shape["cx"] == NX and mesh.shape["cy"] == NZ
    spec = P(("batch", "cy", "cx"), None, None)

    def local(q, k, v):
        t, h, d = q.shape
        pc = t // 2
        rows = NX * pc
        c = d ** -0.5 * math.log2(math.e)
        tq = 2 * pc
        tiles = rows // tq
        f32, bf = jnp.float32, jnp.bfloat16
        dma = pltpu.SemaphoreType.DMA
        ot = pl.pallas_call(
            functools.partial(kernel, c),
            out_shape=jax.ShapeDtypeStruct((h, t, d), bf),
            in_specs=[pl.BlockSpec(memory_space=pl.ANY)] * 3,
            out_specs=pl.BlockSpec(memory_space=pl.ANY),
            scratch_shapes=[
                pltpu.VMEM((5, GQ, rows, d), bf),
                pltpu.VMEM((SLOTS, 2 * NZ, rows, d), bf),
                pltpu.VMEM((SLOTS, 2 * NZ, d, rows), bf),
                pltpu.VMEM((5, GQ * tiles, 1, tq), f32),
                pltpu.VMEM((5, GQ * tiles, 8, tq), f32),
                pltpu.VMEM((5, GQ * tiles, d, tq), f32),
                pltpu.VMEM((5, GQ, rows, d), bf),
                pltpu.VMEM((rows, tq), f32),
                pltpu.VMEM((rows, tq), f32),
                pltpu.VMEM((8, tq), f32),
                pltpu.VMEM((8, tq), f32),
                dma((SLOTS, 3, 2, NX)),
                dma((SLOTS, 3, 3, NX)),
                dma((SLOTS, 3, 2)),
                dma((SLOTS, 2 * NZ, 2)),
                dma((SLOTS, 2 * NZ, 2)),
                dma((SLOTS, 2 * NZ, 2)),
                dma((5, NX)),
                dma((4, NX)),
            ],
            compiler_params=pltpu.CompilerParams(
                collective_id=0, has_side_effects=True, vmem_limit_bytes=56 * 2**20),
        )(jnp.transpose(q, (1, 0, 2)), jnp.transpose(k, (1, 0, 2)), jnp.transpose(v, (1, 2, 0)))
        return jnp.transpose(ot, (1, 0, 2))

    return jax.shard_map(local, mesh=mesh, in_specs=(spec, spec, spec), out_specs=spec, check_vma=False)
```

time: 209 us -> 207 us (level)
  no operation moved by 1% of the time
where the time goes in v2:
time: 207 us
  Pallas kernels  194 us (94%)
  local copies, waits for them, and re-layouts  12.9 us (6%)
    pallas_call x1, Pallas kernels, local(): pl.pallas_call(functools.partial(kernel, c), out_shape=jax.ShapeDtypeStru...  194 us
    unnamed x5, local copies, waits for them, and re-layouts  7.29 us
    transpose x1, local copies, waits for them, and re-layouts, local(): return jnp.transpose(ot, (1, 0, 2))  5.58 us

profile of v2, /device:TPU:0, one launch (start us, length us, event | category | flops | bytes accessed | tf_op | source)
XLA Modules:
  0.0 206.6 jit_solution(9330308678117887531)
XLA Ops:
  0.0 0.0 copy-start
  0.0 2.5 %copy.11 = bf16[512,8,128]{2,0,1:T(8,128)(2,1)} copy(bf16[512,8,128]{2,1,0:T(8,128)(2,1)} %param.4) | data formatting | bytes 2097152 | tf_op args[1]
  2.5 2.4 %copy.6 = bf16[512,8,128]{0,2,1:T(8,128)(2,1)} copy(bf16[512,8,128]{2,1,0:T(8,128)(2,1)} %param.5) | data formatting | bytes 2097152 | tf_op args[2]
  4.9 0.0 copy-done
  4.9 2.4 %copy.10 = bf16[512,24,128]{2,0,1:T(8,128)(2,1)} copy(bf16[512,24,128]{2,1,0:T(8,128)(2,1)S(1)} %copy-done) | data formatting | bytes 6291456 | tf_op args[0]
  7.3 193.7 %shard_map.37 = bf16[24,512,128]{2,1,0:T(8,128)(2,1)} custom-call(bf16[24,512,128]{2,1,0:T(8,128)(2,1)} %bitcast.9, bf16[8,512,128]{2,1,0:T(8,128)(2,1)} %bitcast.10, bf16[8,128,512]{2,1,0:T(8,128)(2,1)} %bitcast.11), custom_call_target="tpu_custom_call" | custom-call | tf_op jit(solution)/shard_map/pallas_call | solution.py:412
  201.0 5.6 %copy.7 = bf16[512,24,128]{2,1,0:T(8,128)(2,1)} copy(bf16[512,24,128]{2,0,1:T(8,128)(2,1)} %bitcast.8) | data formatting | bytes 6291456 | tf_op jit(solution)/shard_map/transpose | solution.py:441
Async XLA Ops:
  0.0 4.9 %copy-start = (bf16[512,24,128]{2,1,0:T(8,128)(2,1)S(1)}, bf16[512,24,128]{2,1,0:T(8,128)(2,1)}, u32[]{:S(2)}) copy-start(bf16[512,24,128]{2,1,0:T(8,128)(2,1)} %param.3) | copy-start | bytes 9437188

commit v3 on v2

v3 whole, which is shorter than its diff:
```python
import functools
import math

import jax
import jax.numpy as jnp
from jax import lax
from jax.experimental import pallas as pl
from jax.experimental.pallas import tpu as pltpu
from jax.sharding import PartitionSpec as P


NX = 4
NZ = 4
SLOTS = 2
GQ = 3
NB = 4
NT = (((1,), (1,)), ((), ()))
MESH = pl.DeviceIdType.MESH
I = jnp.int32


def stage(c, nxt, cur):
    qn, kn_ref, s_nxt, x_nxt, base, rows = nxt
    tq = qn.shape[0]
    bk = kn_ref.shape[0] // NB
    blocks = rows // bk
    if cur is not None:
        s_cur, x_cur, v_ref, m_ref, l_ref, a_ref, keys = cur
        blocks = max(blocks, keys // bk)
        m0 = m_ref[...]
        m1 = jnp.maximum(m0, jnp.max(x_cur[...], axis=0, keepdims=True))
        al = jnp.exp2((m0 - m1) * c)
        m_ref[...] = m1
        lsum = l_ref[...] * al
    xm = o = None
    for b in range(blocks):
        r = slice(b * bk, (b + 1) * bk)
        if b * bk < rows:
            s = lax.dot_general(kn_ref[r, :], qn, NT, preferred_element_type=jnp.float32)
            if base is not None and (b + 1) * bk > base:
                kk = lax.broadcasted_iota(I, s.shape, 0) + b * bk
                qq = lax.broadcasted_iota(I, s.shape, 1) + base
                s = jnp.where(kk <= qq, s, -jnp.inf)
            s_nxt[r, :] = s
            y = jnp.max(s.reshape(bk // 8, 8, tq), axis=0)
            xm = y if xm is None else jnp.maximum(xm, y)
        if cur is not None and b * bk < keys:
            p = jnp.exp2((s_cur[r, :] - m1) * c)
            lsum = lsum + jnp.sum(p.reshape(bk // 8, 8, tq), axis=0)
            d = jnp.dot(v_ref[:, r], p.astype(jnp.bfloat16), preferred_element_type=jnp.float32)
            o = d if o is None else o + d
    x_nxt[...] = xm
    if cur is not None:
        l_ref[...] = lsum
        a_ref[...] = a_ref[...] * al + o


SHIFT = 4
TOP = 2 * NZ - 1
START, QUERY, EXTRA, BELOW, ABOVE = 1, 2, 3, 4, 5
RADIX = (5, 2, 8, 2, 6, 2, 2, 4)


def units(z):
    out = []

    def add(qs, ch, masked=0, act=0):
        out.append((qs, 1 if qs == SHIFT else qs // 2, ch, masked, act))

    def own(g, act):
        add(2 * g, z, 1, act)
        if not (g == 1 and z == 0):
            add(2 * g + 1, TOP - z, 1)
            add(2 * g + 1, z)

    own(0, START)
    for t in range(1, NZ):
        if z >= t:
            add(0, z - t, 0, BELOW)
            add(1, z - t)
        if z + t < NZ:
            add(1, z + t, 0, ABOVE)
            add(1, TOP - z - t, 0, ABOVE)
        if z == 0 and t == 1:
            own(1, QUERY)
    if z > 0:
        own(1, QUERY)
        add(SHIFT, z, 0, EXTRA)
        add(SHIFT, TOP - z)
        for t in range(1, NZ):
            if z >= t:
                add(SHIFT, z - t, 0, BELOW)
                add(2, z - t)
                add(3, z - t)
                add(SHIFT, TOP - z + t, int(z == t), BELOW)
            if z + t < NZ:
                for ch in (z + t, TOP - z - t):
                    add(SHIFT, ch, 0, ABOVE)
                    add(3, ch)
    last = {u[0]: i for i, u in enumerate(out)}
    return [u + (int(i == 3), int(last[u[0]] == i), 1 if u[0] == SHIFT else GQ) for i, u in enumerate(out)]


def pack(u):
    x = 0
    for r, f in zip(RADIX, u):
        x = x * r + f
    return x


def unpack(x):
    out = []
    for r in RADIX[::-1]:
        out.append(lax.rem(x, I(r)))
        x = lax.div(x, I(r))
    return out[::-1]


def kernel(c, q, k, v, o, qb, kb, vb, m, l, a, ost, sa, sb, xa, xb,
           xsend, xrecv, xloc, qsend, qrecv, zrecv, dsend, usend, osend, orecv):
    z = lax.axis_index("cy")
    j = lax.axis_index("cx")
    pc = k.shape[1] // 2
    tq = sa.shape[1]
    tiles = qb.shape[2] // tq

    def mod(x):
        return lax.rem(x + 2 * NX, I(NX))

    def chunk(part):
        return z if part == 0 else TOP - z

    def pos(part, jj):
        return jj if part == 0 else NX - 1 - jj

    def span(part, jj):
        return pl.ds(pl.multiple_of(pos(part, jj) * pc, pc), pc)

    barrier = pltpu.get_barrier_semaphore()
    for p in range(1, NX):
        pl.semaphore_signal(barrier, inc=1, device_id={"cx": mod(j + p)}, device_id_type=MESH)

    @pl.when(z > 1)
    def _():
        pl.semaphore_signal(barrier, inc=1, device_id={"cy": z - 1}, device_id_type=MESH)

    @pl.when((z > 0) & (z < NZ - 1))
    def _():
        pl.semaphore_signal(barrier, inc=1, device_id={"cy": z + 1}, device_id_type=MESH)

    for p in range(NX):
        @pl.when(z > 0)
        def _():
            pl.semaphore_signal(barrier, inc=1, device_id={"cy": I(0), "cx": mod(j + p)}, device_id_type=MESH)

        @pl.when(z == 0)
        def _():
            for zz in range(1, NZ):
                pl.semaphore_signal(barrier, inc=1, device_id={"cy": I(zz), "cx": mod(j + p)}, device_id_type=MESH)

    def by_z(values):
        x = I(values[-1])
        for zz in range(NZ - 1):
            x = jnp.where(z == zz, I(values[zz]), x)
        return x

    lists = [[pack(u) for u in units(zz)] for zz in range(NZ)]
    count = by_z([len(x) for x in lists])
    codes = [by_z([x[min(i, len(x) - 1)] for x in lists]) for i in range(max(map(len, lists)))]

    def fields(u):
        x = codes[-1]
        for i, code in enumerate(codes[:-1]):
            x = jnp.where(u == i, code, x)
        return unpack(x)

    pl.semaphore_wait(barrier, NX - 1 + by_z([NX * (NZ - 1)] + [NX + 2] * (NZ - 2) + [NX + 1]) - jnp.where(z == 1, 1, 0))

    def pair(g, kind, part, owner, dest):
        half = pl.ds(part * pc, pc)
        at = span(part, owner)
        if kind == 0:
            return k.at[SLOTS * dest + g, half, :], kb.at[g, chunk(part), at, :]
        if kind == 1:
            return v.at[SLOTS * dest + g, :, half], vb.at[g, chunk(part), :, at]
        return q.at[pl.ds(GQ * (SLOTS * dest + g), GQ), half, :], qb.at[2 * g + part, :, at, :]

    def xcopy(g, kind, part, p, owner, dest):
        src, dst = pair(g, kind, part, owner, dest)
        return pltpu.make_async_remote_copy(
            src_ref=src, dst_ref=dst, send_sem=xsend.at[g, kind, part, p - 1], recv_sem=xrecv.at[g, kind, part, p - 1],
            device_id={"cx": dest}, device_id_type=MESH)

    def xlocal(g, kind, part):
        src, dst = pair(g, kind, part, j, j)
        return pltpu.make_async_copy(src, dst, xloc.at[g, kind, part])

    for g in range(SLOTS):
        for kinds in ((0, 1), (2,)):
            for part in range(2):
                for p in range(1, NX):
                    for kind in kinds:
                        xcopy(g, kind, part, p, j, mod(j + p)).start()
                for kind in kinds:
                    xlocal(g, kind, part).start()

    def xwait(g, kinds):
        for part in range(2):
            for kind in kinds:
                xlocal(g, kind, part).wait()
                for p in range(1, NX):
                    xcopy(g, kind, part, p, mod(j - p), j).wait_recv()

    def shift(zz):
        return pltpu.make_async_remote_copy(
            src_ref=qb.at[3, zz - 1], dst_ref=qb.at[SHIFT, 0], send_sem=qsend.at[zz - 1], recv_sem=qrecv.at[0],
            device_id={"cy": I(zz)}, device_id_type=MESH)

    def zcopies(g, ch, dz, send):
        return [
            pltpu.make_async_remote_copy(
                src_ref=buf.at[g, ch], dst_ref=buf.at[g, ch], send_sem=send.at[g, ch, i], recv_sem=zrecv.at[g, ch, i],
                device_id={"cy": z + dz}, device_id_type=MESH)
            for i, buf in enumerate((kb, vb))
        ]

    def goes_down(g):
        return z > jnp.where(g == 1, 1, 0)

    def down(g, ch):
        @pl.when(goes_down(g))
        def _():
            for d in zcopies(g, ch, -1, dsend):
                d.start()

    def up(g, ch):
        @pl.when(z < NZ - 1)
        def _():
            for d in zcopies(g, ch, 1, usend):
                d.start()

    m[...] = jnp.full_like(m, -jnp.inf)
    l[...] = jnp.zeros_like(l)

    @pl.loop(0, 5)
    def _(i):
        a[i] = jnp.zeros(a.shape[1:], a.dtype)

    def before(f):
        _, g, ch, _, act, kv, _, _ = f

        def begin(g):
            xwait(g, (0, 1))
            for ch in (z, TOP - z):
                down(I(g), ch)
            up(I(g), z)
            if g == 1:
                up(I(g), TOP - z)

        pl.when(kv == 1)(lambda: begin(1))

        @pl.when(act == START)
        def _():
            begin(0)
            xwait(0, (2,))

        @pl.when(act == QUERY)
        def _():
            xwait(1, (2,))

            @pl.when(z == 0)
            def _():
                for zz in range(1, NZ):
                    shift(zz).start()

        @pl.when(act == EXTRA)
        def _():
            shift(1).wait_recv()

        @pl.when(act == BELOW)
        def _():
            for d in zcopies(g, ch, 1, usend):
                d.wait_recv()
            up(g, ch)

        @pl.when(act == ABOVE)
        def _():
            for d in zcopies(g, ch, -1, dsend):
                d.wait_recv()
            down(g, ch)

    def opiece(g, part, owner, dest, heads, hd, shifted):
        qs, to = (SHIFT, hd + z - 1) if shifted else (2 * g + part, hd)
        return dict(
            src_ref=ost.at[qs, pl.ds(hd, heads), span(part, dest), :],
            dst_ref=o.at[pl.ds(GQ * (SLOTS * owner + g) + to, heads), pl.ds(part * pc, pc), :])

    def oremote(g, part, p, owner, dest, heads=GQ, hd=0, shifted=False):
        return pltpu.make_async_remote_copy(
            **opiece(g, part, owner, dest, heads, hd, shifted),
            send_sem=osend.at[SHIFT if shifted else 2 * g + part, p], recv_sem=orecv.at[2 * g + part, p],
            device_id={"cy": I(0) if shifted else z, "cx": dest}, device_id_type=MESH)

    def olocal(g, part, heads=GQ, hd=0):
        r = opiece(g, part, j, j, heads, hd, False)
        return pltpu.make_async_copy(r["src_ref"], r["dst_ref"], osend.at[2 * g + part, 0])

    def finish(qs, n):
        y = a[qs, n] / jnp.sum(l[qs, n], axis=0, keepdims=True)
        at = pl.ds(pl.multiple_of(lax.rem(n, I(tiles)) * tq, tq), tq)
        ost[qs, lax.div(n, I(tiles)), at, :] = y.astype(ost.dtype).T

    def give_back(qs, n):
        hd = lax.div(n, I(tiles))
        for case in range(5):
            @pl.when(qs == case)
            def _():
                shifted = case == SHIFT
                g, part = (1, 1) if shifted else (case // 2, case % 2)
                for e in range(tq // pc):
                    at = lax.rem(n, I(tiles)) * (tq // pc) + e
                    dest = pos(part, at)
                    p = mod(dest - j)
                    if shifted:
                        oremote(g, part, p, j, dest, 1, hd, True).start()
                    else:
                        pl.when(p == 0)(lambda: olocal(g, part, 1, hd).start())
                        pl.when(p > 0)(lambda: oremote(g, part, p, j, dest, 1, hd).start())

    def after(f, n, w, nw):
        pl.when(f[6] == 1)(lambda: finish(f[0], n))
        pl.when(w[6] == 1)(lambda: give_back(w[0], nw))

    def nxt(f, n, s, x, odd, masked):
        at = pl.ds(odd * tq, tq)
        rows = kb.shape[2] if odd or not masked else tq
        return (qb[f[0], lax.div(I(n), I(tiles)), at, :], kb.at[f[1], f[2]], s, x, odd * tq if masked else None, rows)

    def step(fn, nn, s_n, x_n, f, n, s_c, x_c, odd):
        qs = f[0]
        for masked in (False, True):
            @pl.when(fn[3] == int(masked))
            def _():
                keys = tq if odd and masked else kb.shape[2]
                stage(c, nxt(fn, nn, s_n, x_n, odd, masked),
                      (s_c, x_c, vb.at[f[1], f[2]], m.at[qs, n], l.at[qs, n], a.at[qs, n], keys))

    first = fields(I(0))
    before(first)
    stage(c, nxt(first, 0, sa, xa, 0, True), None)

    @pl.loop(0, count)
    def _(u):
        f = fields(u)
        fn = fields(jnp.minimum(u + 1, count - 1))
        w = fields(jnp.maximum(u - 1, 0))
        w[6] = jnp.where(u > 0, w[6], 0)

        @pl.loop(0, f[7])
        def _(i):
            n = tiles * i
            step(f, n + 1, sb, xb, f, n, sa, xa, 1)
            after(f, n, [jnp.where(i == 0, p, q) for p, q in zip(w, f)], jnp.where(i == 0, tiles * w[7] - 1, n - 1))
            wrap = i == f[7] - 1
            pl.when(wrap & (u + 1 < count))(lambda: before(fn))
            step([jnp.where(wrap, p, q) for p, q in zip(fn, f)], jnp.where(wrap, 0, n + 2), sa, xa, f, n + 1, sb, xb, 0)
            after(f, n + 1, f, n)

    for g in range(SLOTS):
        for part in range(2):
            for p in range(1, NX):
                for kind in range(3):
                    xcopy(g, kind, part, p, j, mod(j + p)).wait_send()
    end = fields(count - 1)
    give_back(end[0], tiles * end[7] - 1)
    for g in range(SLOTS):
        for s in range(NZ):
            @pl.when(goes_down(g) & (s >= z))
            def _():
                for ch in (s, TOP - s):
                    for d in zcopies(g, ch, -1, dsend):
                        d.wait_send()

            @pl.when((z < NZ - 1) & (s <= z))
            def _():
                for ch in (s,) if g == 0 else (s, TOP - s):
                    for d in zcopies(g, ch, 1, usend):
                        d.wait_send()
        for part in range(2):
            def keep():
                olocal(g, part).wait()
                for p in range(1, NX):
                    oremote(g, part, p, j, mod(j + p)).wait_send()
                    oremote(g, part, p, mod(j - p), j).wait_recv()

            def given():
                for p in range(NX):
                    oremote(g, part, p, mod(j - p), j).wait_recv()

            if g == 1 and part == 1:
                pl.when(z == 0)(given)
                pl.when(z > 0)(keep)
            else:
                keep()

    @pl.when(z == 0)
    def _():
        for zz in range(1, NZ):
            shift(zz).wait_send()

    @pl.when(z > 0)
    def _():
        for p in range(NX):
            oremote(1, 1, p, j, mod(j + p), 1, shifted=True).wait_send()


def solution(mesh):
    assert mesh.shape["cx"] == NX and mesh.shape["cy"] == NZ
    spec = P(("batch", "cy", "cx"), None, None)

    def local(q, k, v):
        t, h, d = q.shape
        pc = t // 2
        rows = NX * pc
        c = d ** -0.5 * math.log2(math.e)
        tq = 2 * pc
        tiles = rows // tq
        f32, bf = jnp.float32, jnp.bfloat16
        dma = pltpu.SemaphoreType.DMA
        ot = pl.pallas_call(
            functools.partial(kernel, c),
            out_shape=jax.ShapeDtypeStruct((h, t, d), bf),
            in_specs=[pl.BlockSpec(memory_space=pl.ANY)] * 3,
            out_specs=pl.BlockSpec(memory_space=pl.ANY),
            scratch_shapes=[
                pltpu.VMEM((5, GQ, rows, d), bf),
                pltpu.VMEM((SLOTS, 2 * NZ, rows, d), bf),
                pltpu.VMEM((SLOTS, 2 * NZ, d, rows), bf),
                pltpu.VMEM((5, GQ * tiles, 1, tq), f32),
                pltpu.VMEM((5, GQ * tiles, 8, tq), f32),
                pltpu.VMEM((5, GQ * tiles, d, tq), f32),
                pltpu.VMEM((5, GQ, rows, d), bf),
                pltpu.VMEM((rows, tq), f32),
                pltpu.VMEM((rows, tq), f32),
                pltpu.VMEM((8, tq), f32),
                pltpu.VMEM((8, tq), f32),
                dma((SLOTS, 3, 2, NX - 1)),
                dma((SLOTS, 3, 2, NX - 1)),
                dma((SLOTS, 3, 2)),
                dma((NZ - 1,)),
                dma((1,)),
                dma((SLOTS, 2 * NZ, 2)),
                dma((SLOTS, 2 * NZ, 2)),
                dma((SLOTS, 2 * NZ, 2)),
                dma((5, NX)),
                dma((4, NX)),
            ],
            compiler_params=pltpu.CompilerParams(
                collective_id=0, has_side_effects=True, vmem_limit_bytes=56 * 2**20),
        )(jnp.transpose(q, (1, 0, 2)), jnp.transpose(k, (1, 0, 2)), jnp.transpose(v, (1, 2, 0)))
        return jnp.transpose(ot, (1, 0, 2))

    return jax.shard_map(local, mesh=mesh, in_specs=(spec, spec, spec), out_specs=spec, check_vma=False)
```

time: 207 us -> 187 us (0.903)
  Pallas kernels: 194 us -> 174 us
    pallas_call x1, Pallas kernels: 194 us -> 174 us  [local(): pl.pallas_call(functools.partial(kernel, c), out_shape=jax.ShapeDtypeStru...]
where the time goes in v3:
time: 187 us
  Pallas kernels  174 us (93%)
  local copies, waits for them, and re-layouts  12.9 us (7%)
    pallas_call x1, Pallas kernels, local(): pl.pallas_call(functools.partial(kernel, c), out_shape=jax.ShapeDtypeStru...  174 us
    unnamed x5, local copies, waits for them, and re-layouts  7.29 us
    transpose x1, local copies, waits for them, and re-layouts, local(): return jnp.transpose(ot, (1, 0, 2))  5.58 us

profile of v3, /device:TPU:0, one launch (start us, length us, event | category | flops | bytes accessed | tf_op | source)
XLA Modules:
  0.0 187.0 jit_solution(16153892860108925890)
XLA Ops:
  0.0 0.0 copy-start
  0.0 2.5 %copy.11 = bf16[512,8,128]{2,0,1:T(8,128)(2,1)} copy(bf16[512,8,128]{2,1,0:T(8,128)(2,1)} %param.4) | data formatting | bytes 2097152 | tf_op args[1]
  2.5 2.4 %copy.6 = bf16[512,8,128]{0,2,1:T(8,128)(2,1)} copy(bf16[512,8,128]{2,1,0:T(8,128)(2,1)} %param.5) | data formatting | bytes 2097152 | tf_op args[2]
  4.9 0.0 copy-done
  4.9 2.4 %copy.10 = bf16[512,24,128]{2,0,1:T(8,128)(2,1)} copy(bf16[512,24,128]{2,1,0:T(8,128)(2,1)S(1)} %copy-done) | data formatting | bytes 6291456 | tf_op args[0]
  7.3 174.1 %shard_map.37 = bf16[24,512,128]{2,1,0:T(8,128)(2,1)} custom-call(bf16[24,512,128]{2,1,0:T(8,128)(2,1)} %bitcast.9, bf16[8,512,128]{2,1,0:T(8,128)(2,1)} %bitcast.10, bf16[8,128,512]{2,1,0:T(8,128)(2,1)} %bitcast.11), custom_call_target="tpu_custom_call" | custom-call | tf_op jit(solution)/shard_map/pallas_call | solution.py:430
  181.4 5.6 %copy.7 = bf16[512,24,128]{2,1,0:T(8,128)(2,1)} copy(bf16[512,24,128]{2,0,1:T(8,128)(2,1)} %bitcast.8) | data formatting | bytes 6291456 | tf_op jit(solution)/shard_map/transpose | solution.py:461
Async XLA Ops:
  0.0 4.9 %copy-start = (bf16[512,24,128]{2,1,0:T(8,128)(2,1)S(1)}, bf16[512,24,128]{2,1,0:T(8,128)(2,1)}, u32[]{:S(2)}) copy-start(bf16[512,24,128]{2,1,0:T(8,128)(2,1)} %param.3) | copy-start | bytes 9437188

commit v4 on v3

--- a/solution.py
+++ b/solution.py
@@ -56,49 +56,36 @@
 
 
 SHIFT = 4
+SHARE = {1: (0, 2), 2: (2, 1)}
+FAR = max(SHARE)
 TOP = 2 * NZ - 1
-START, QUERY, EXTRA, BELOW, ABOVE = 1, 2, 3, 4, 5
-RADIX = (5, 2, 8, 2, 6, 2, 2, 4)
-
+KV1, QUERY, EXTRA, LAND = 1, 2, 3, 4
+RADIX = (5, 2, 8, 2, 2, 4, 2, 20, 20, 20)
+
+ORDER = (
+    ((0, 0, 5), (1, 7), (1, 0), (1, 1, 10), (1, 6, 1), (1, 2, 6), (2, 0, 2), (1, 5, 9), (1, 3, 7), (1, 4, 8)),
+    ((0, 1, 4, 6), (0, 0), (1, 6, 9), (1, 0), (1, 1, 1), (1, 2), (1, 3, 7), (1, 5), (1, 4, 12, 2, 8), (2, 1), (2, 0),
+     (3, 6, 19), (3, 0, 14), (3, 1), (4, 7, 3), (4, 0, 17), (4, 1), (4, 2), (4, 5), (4, 3, 15), (4, 6), (3, 2), (3, 3),
+     (4, 4, 16), (3, 4), (3, 5)),
+    ((0, 2, 5, 7), (0, 1), (1, 5, 8), (1, 1), (0, 0, 1, 4), (1, 0), (1, 2), (1, 3), (1, 4, 13, 15, 2), (2, 2), (2, 1),
+     (3, 5, 16, 18), (3, 1), (3, 2), (3, 3), (3, 4), (4, 1, 3), (4, 2), (4, 3), (4, 4), (4, 5), (4, 6), (4, 0, 12), (2, 0),
+     (3, 0), (4, 7, 19)),
+    ((0, 3, 6), (0, 2), (1, 4), (1, 2), (0, 1, 1, 5), (1, 1), (1, 3), (2, 3, 14, 2), (2, 2), (3, 4), (0, 0, 4), (1, 0), (3, 2),
+     (2, 1, 13), (3, 1), (3, 3), (2, 0, 12), (3, 0)),
+)
 
 def units(z):
     out = []
-
-    def add(qs, ch, masked=0, act=0):
-        out.append((qs, 1 if qs == SHIFT else qs // 2, ch, masked, act))
-
-    def own(g, act):
-        add(2 * g, z, 1, act)
-        if not (g == 1 and z == 0):
-            add(2 * g + 1, TOP - z, 1)
-            add(2 * g + 1, z)
-
-    own(0, START)
-    for t in range(1, NZ):
-        if z >= t:
-            add(0, z - t, 0, BELOW)
-            add(1, z - t)
-        if z + t < NZ:
-            add(1, z + t, 0, ABOVE)
-            add(1, TOP - z - t, 0, ABOVE)
-        if z == 0 and t == 1:
-            own(1, QUERY)
-    if z > 0:
-        own(1, QUERY)
-        add(SHIFT, z, 0, EXTRA)
-        add(SHIFT, TOP - z)
-        for t in range(1, NZ):
-            if z >= t:
-                add(SHIFT, z - t, 0, BELOW)
-                add(2, z - t)
-                add(3, z - t)
-                add(SHIFT, TOP - z + t, int(z == t), BELOW)
-            if z + t < NZ:
-                for ch in (z + t, TOP - z - t):
-                    add(SHIFT, ch, 0, ABOVE)
-                    add(3, ch)
-    last = {u[0]: i for i, u in enumerate(out)}
-    return [u + (int(i == 3), int(last[u[0]] == i), 1 if u[0] == SHIFT else GQ) for i, u in enumerate(out)]
+    steps = 0
+    work = ORDER[z]
+    last = {u[0]: i for i, u in enumerate(work)}
+    for i, (qs, ch, *acts) in enumerate(work):
+        heads = SHARE[z][1] if qs == SHIFT else GQ
+        diagonal = TOP if qs == SHIFT else z if qs % 2 == 0 else TOP - z
+        out.append((qs, 1 if qs == SHIFT else qs // 2, ch, int(ch == diagonal), int(last[qs] == i), heads, steps % 2,
+                    *acts, *[0] * (3 - len(acts))))
+        steps += heads
+    return out
 
 
 def pack(u):
@@ -121,7 +108,7 @@
     z = lax.axis_index("cy")
     j = lax.axis_index("cx")
     pc = k.shape[1] // 2
-    tq = sa.shape[1]
+    tq = sa.shape[2]
     tiles = qb.shape[2] // tq
 
     def mod(x):
@@ -149,13 +136,13 @@
         pl.semaphore_signal(barrier, inc=1, device_id={"cy": z + 1}, device_id_type=MESH)
 
     for p in range(NX):
-        @pl.when(z > 0)
+        @pl.when((z > 0) & (z <= FAR))
         def _():
             pl.semaphore_signal(barrier, inc=1, device_id={"cy": I(0), "cx": mod(j + p)}, device_id_type=MESH)
 
         @pl.when(z == 0)
         def _():
-            for zz in range(1, NZ):
+            for zz in SHARE:
                 pl.semaphore_signal(barrier, inc=1, device_id={"cy": I(zz), "cx": mod(j + p)}, device_id_type=MESH)
 
     def by_z(values):
@@ -174,7 +161,7 @@
             x = jnp.where(u == i, code, x)
         return unpack(x)
 
-    pl.semaphore_wait(barrier, NX - 1 + by_z([NX * (NZ - 1)] + [NX + 2] * (NZ - 2) + [NX + 1]) - jnp.where(z == 1, 1, 0))
+    pl.semaphore_wait(barrier, NX - 1 + by_z([NX * FAR, NX + 1, NX + 2, 1]))
 
     def pair(g, kind, part, owner, dest):
         half = pl.ds(part * pc, pc)
@@ -213,7 +200,7 @@
 
     def shift(zz):
         return pltpu.make_async_remote_copy(
-            src_ref=qb.at[3, zz - 1], dst_ref=qb.at[SHIFT, 0], send_sem=qsend.at[zz - 1], recv_sem=qrecv.at[0],
+            src_ref=qb.at[3, pl.ds(*SHARE[zz])], dst_ref=qb.at[SHIFT, pl.ds(0, SHARE[zz][1])], send_sem=qsend.at[zz - 1], recv_sem=qrecv.at[0],
             device_id={"cy": I(zz)}, device_id_type=MESH)
 
     def zcopies(g, ch, dz, send):
@@ -234,7 +221,7 @@
                 d.start()
 
     def up(g, ch):
-        @pl.when(z < NZ - 1)
+        @pl.when(z < jnp.where(ch < NZ, NZ - 1, FAR))
         def _():
             for d in zcopies(g, ch, 1, usend):
                 d.start()
@@ -246,51 +233,54 @@
     def _(i):
         a[i] = jnp.zeros(a.shape[1:], a.dtype)
 
+    def begin(g):
+        xwait(g, (0, 1))
+        for ch in (z, TOP - z):
+            down(I(g), ch)
+        up(I(g), z)
+        if g == 1:
+            up(I(g), TOP - z)
+
     def before(f):
-        _, g, ch, _, act, kv, _, _ = f
-
-        def begin(g):
-            xwait(g, (0, 1))
-            for ch in (z, TOP - z):
-                down(I(g), ch)
-            up(I(g), z)
-            if g == 1:
-                up(I(g), TOP - z)
-
-        pl.when(kv == 1)(lambda: begin(1))
-
-        @pl.when(act == START)
-        def _():
-            begin(0)
-            xwait(0, (2,))
-
-        @pl.when(act == QUERY)
-        def _():
-            xwait(1, (2,))
-
-            @pl.when(z == 0)
-            def _():
-                for zz in range(1, NZ):
-                    shift(zz).start()
-
-        @pl.when(act == EXTRA)
-        def _():
-            shift(1).wait_recv()
-
-        @pl.when(act == BELOW)
-        def _():
-            for d in zcopies(g, ch, 1, usend):
-                d.wait_recv()
-            up(g, ch)
-
-        @pl.when(act == ABOVE)
-        def _():
-            for d in zcopies(g, ch, -1, dsend):
-                d.wait_recv()
-            down(g, ch)
+        @pl.loop(0, 3)
+        def _(i):
+            act = jnp.where(i == 0, f[7], jnp.where(i == 1, f[8], f[9]))
+            pl.when(act == KV1)(lambda: begin(1))
+
+            @pl.when(act == QUERY)
+            def _():
+                xwait(1, (2,))
+
+                @pl.when(z == 0)
+                def _():
+                    for zz in SHARE:
+                        shift(zz).start()
+
+            @pl.when(act == EXTRA)
+            def _():
+                for zz in SHARE:
+                    pl.when(z == zz)(lambda: shift(zz).wait_recv())
+
+            @pl.when(act >= LAND)
+            def _():
+                g = lax.div(act - LAND, I(2 * NZ))
+                ch = lax.rem(jnp.maximum(act - LAND, 0), I(2 * NZ))
+                source = jnp.where(ch < NZ, ch, TOP - ch)
+
+                @pl.when(source < z)
+                def _():
+                    for d in zcopies(g, ch, 1, usend):
+                        d.wait_recv()
+                    up(g, ch)
+
+                @pl.when(source > z)
+                def _():
+                    for d in zcopies(g, ch, -1, dsend):
+                        d.wait_recv()
+                    down(g, ch)
 
     def opiece(g, part, owner, dest, heads, hd, shifted):
-        qs, to = (SHIFT, hd + z - 1) if shifted else (2 * g + part, hd)
+        qs, to = (SHIFT, hd + 2 * (z - 1)) if shifted else (2 * g + part, hd)
         return dict(
             src_ref=ost.at[qs, pl.ds(hd, heads), span(part, dest), :],
             dst_ref=o.at[pl.ds(GQ * (SLOTS * owner + g) + to, heads), pl.ds(part * pc, pc), :])
@@ -327,44 +317,59 @@
                         pl.when(p == 0)(lambda: olocal(g, part, 1, hd).start())
                         pl.when(p > 0)(lambda: oremote(g, part, p, j, dest, 1, hd).start())
 
-    def after(f, n, w, nw):
-        pl.when(f[6] == 1)(lambda: finish(f[0], n))
-        pl.when(w[6] == 1)(lambda: give_back(w[0], nw))
-
-    def nxt(f, n, s, x, odd, masked):
-        at = pl.ds(odd * tq, tq)
-        rows = kb.shape[2] if odd or not masked else tq
-        return (qb[f[0], lax.div(I(n), I(tiles)), at, :], kb.at[f[1], f[2]], s, x, odd * tq if masked else None, rows)
-
-    def step(fn, nn, s_n, x_n, f, n, s_c, x_c, odd):
+    def after(f, h, w, hw):
+        @pl.when(f[4] == 1)
+        def _():
+            for e in range(tiles):
+                finish(f[0], tiles * h + e)
+
+        @pl.when(w[4] == 1)
+        def _():
+            for e in range(tiles):
+                give_back(w[0], tiles * hw + e)
+
+    bufs = ((sa, xa), (sb, xb))
+
+    def nxt(f, h, e, par, masked):
+        rows = (e + 1) * tq if masked else kb.shape[2]
+        sx, xx = bufs[par]
+        return qb[f[0], h, pl.ds(e * tq, tq), :], kb.at[f[1], f[2]], sx.at[e], xx.at[e], e * tq if masked else None, rows
+
+    def step(fn, hn, f, h):
         qs = f[0]
-        for masked in (False, True):
-            @pl.when(fn[3] == int(masked))
-            def _():
-                keys = tq if odd and masked else kb.shape[2]
-                stage(c, nxt(fn, nn, s_n, x_n, odd, masked),
-                      (s_c, x_c, vb.at[f[1], f[2]], m.at[qs, n], l.at[qs, n], a.at[qs, n], keys))
+        parity = lax.rem(f[6] + h, I(2))
+        for par in range(2):
+            for m_cur in (False, True):
+                for m_nxt in (False, True):
+                    @pl.when((parity == par) & (f[3] == int(m_cur)) & (fn[3] == int(m_nxt)))
+                    def _():
+                        for e in range(tiles):
+                            n = tiles * h + e
+                            sx, xx = bufs[par]
+                            keys = (e + 1) * tq if m_cur else kb.shape[2]
+                            stage(c, nxt(fn, hn, e, 1 - par, m_nxt),
+                                  (sx.at[e], xx.at[e], vb.at[f[1], f[2]], m.at[qs, n], l.at[qs, n], a.at[qs, n], keys))
 
     first = fields(I(0))
+    begin(0)
+    xwait(0, (2,))
     before(first)
-    stage(c, nxt(first, 0, sa, xa, 0, True), None)
+    for e in range(tiles):
+        stage(c, nxt(first, 0, e, 0, True), None)
 
     @pl.loop(0, count)
     def _(u):
         f = fields(u)
         fn = fields(jnp.minimum(u + 1, count - 1))
         w = fields(jnp.maximum(u - 1, 0))
-        w[6] = jnp.where(u > 0, w[6], 0)
-
-        @pl.loop(0, f[7])
-        def _(i):
-            n = tiles * i
-            step(f, n + 1, sb, xb, f, n, sa, xa, 1)
-            after(f, n, [jnp.where(i == 0, p, q) for p, q in zip(w, f)], jnp.where(i == 0, tiles * w[7] - 1, n - 1))
-            wrap = i == f[7] - 1
+        w[4] = jnp.where(u > 0, w[4], 0)
+
+        @pl.loop(0, f[5])
+        def _(h):
+            wrap = h == f[5] - 1
             pl.when(wrap & (u + 1 < count))(lambda: before(fn))
-            step([jnp.where(wrap, p, q) for p, q in zip(fn, f)], jnp.where(wrap, 0, n + 2), sa, xa, f, n + 1, sb, xb, 0)
-            after(f, n + 1, f, n)
+            step([jnp.where(wrap, p, q) for p, q in zip(fn, f)], jnp.where(wrap, 0, h + 1), f, h)
+            after(f, h, [jnp.where(h == 0, p, q) for p, q in zip(w, f)], jnp.where(h == 0, w[5] - 1, h - 1))
 
     for g in range(SLOTS):
         for part in range(2):
@@ -372,7 +377,8 @@
                 for kind in range(3):
                     xcopy(g, kind, part, p, j, mod(j + p)).wait_send()
     end = fields(count - 1)
-    give_back(end[0], tiles * end[7] - 1)
+    for e in range(tiles):
+        give_back(end[0], tiles * (end[5] - 1) + e)
     for g in range(SLOTS):
         for s in range(NZ):
             @pl.when(goes_down(g) & (s >= z))
@@ -383,8 +389,13 @@
 
             @pl.when((z < NZ - 1) & (s <= z))
             def _():
-                for ch in (s,) if g == 0 else (s, TOP - s):
-                    for d in zcopies(g, ch, 1, usend):
+                for d in zcopies(g, s, 1, usend):
+                    d.wait_send()
+
+            if g == 1:
+                @pl.when((z < FAR) & (s <= z))
+                def _():
+                    for d in zcopies(g, TOP - s, 1, usend):
                         d.wait_send()
         for part in range(2):
             def keep():
@@ -405,13 +416,14 @@
 
     @pl.when(z == 0)
     def _():
-        for zz in range(1, NZ):
+        for zz in SHARE:
             shift(zz).wait_send()
 
-    @pl.when(z > 0)
-    def _():
-        for p in range(NX):
-            oremote(1, 1, p, j, mod(j + p), 1, shifted=True).wait_send()
+    for zz in SHARE:
+        @pl.when(z == zz)
+        def _():
+            for p in range(NX):
+                oremote(1, 1, p, j, mod(j + p), SHARE[zz][1], shifted=True).wait_send()
 
 
 def solution(mesh):
@@ -440,10 +452,10 @@
                 pltpu.VMEM((5, GQ * tiles, 8, tq), f32),
                 pltpu.VMEM((5, GQ * tiles, d, tq), f32),
                 pltpu.VMEM((5, GQ, rows, d), bf),
-                pltpu.VMEM((rows, tq), f32),
-                pltpu.VMEM((rows, tq), f32),
-                pltpu.VMEM((8, tq), f32),
-                pltpu.VMEM((8, tq), f32),
+                pltpu.VMEM((tiles, rows, tq), f32),
+                pltpu.VMEM((tiles, rows, tq), f32),
+                pltpu.VMEM((tiles, 8, tq), f32),
+                pltpu.VMEM((tiles, 8, tq), f32),
                 dma((SLOTS, 3, 2, NX - 1)),
                 dma((SLOTS, 3, 2, NX - 1)),
                 dma((SLOTS, 3, 2)),

time: 187 us -> 153 us (0.82)
  Pallas kernels: 174 us -> 140 us
    pallas_call x1, Pallas kernels: 174 us -> 140 us  [local(): pl.pallas_call(functools.partial(kernel, c), out_shape=jax.ShapeDtypeStru...]
where the time goes in v4:
time: 153 us; the launch traced here: 152 us
  Pallas kernels  140 us (92%)
  local copies, waits for them, and re-layouts  12.9 us (8%)
    pallas_call x1, Pallas kernels, local(): pl.pallas_call(functools.partial(kernel, c), out_shape=jax.ShapeDtypeStru...  140 us
    unnamed x5, local copies, waits for them, and re-layouts  7.29 us
    transpose x1, local copies, waits for them, and re-layouts, local(): return jnp.transpose(ot, (1, 0, 2))  5.58 us

profile of v4, /device:TPU:0, one launch (start us, length us, event | category | flops | bytes accessed | tf_op | source)
XLA Modules:
  0.0 152.4 jit_solution(5531978562819265866)
XLA Ops:
  0.0 0.0 copy-start
  0.0 2.5 %copy.11 = bf16[512,8,128]{2,0,1:T(8,128)(2,1)} copy(bf16[512,8,128]{2,1,0:T(8,128)(2,1)} %param.4) | data formatting | bytes 2097152 | tf_op args[1]
  2.5 2.4 %copy.6 = bf16[512,8,128]{0,2,1:T(8,128)(2,1)} copy(bf16[512,8,128]{2,1,0:T(8,128)(2,1)} %param.5) | data formatting | bytes 2097152 | tf_op args[2]
  4.9 0.0 copy-done
  4.9 2.4 %copy.10 = bf16[512,24,128]{2,0,1:T(8,128)(2,1)} copy(bf16[512,24,128]{2,1,0:T(8,128)(2,1)S(1)} %copy-done) | data formatting | bytes 6291456 | tf_op args[0]
  7.3 139.5 %shard_map.37 = bf16[24,512,128]{2,1,0:T(8,128)(2,1)} custom-call(bf16[24,512,128]{2,1,0:T(8,128)(2,1)} %bitcast.9, bf16[8,512,128]{2,1,0:T(8,128)(2,1)} %bitcast.10, bf16[8,128,512]{2,1,0:T(8,128)(2,1)} %bitcast.11), custom_call_target="tpu_custom_call" | custom-call | tf_op jit(solution)/shard_map/pallas_call | solution.py:442
  146.9 5.6 %copy.7 = bf16[512,24,128]{2,1,0:T(8,128)(2,1)} copy(bf16[512,24,128]{2,0,1:T(8,128)(2,1)} %bitcast.8) | data formatting | bytes 6291456 | tf_op jit(solution)/shard_map/transpose | solution.py:473
Async XLA Ops:
  0.0 4.9 %copy-start = (bf16[512,24,128]{2,1,0:T(8,128)(2,1)S(1)}, bf16[512,24,128]{2,1,0:T(8,128)(2,1)}, u32[]{:S(2)}) copy-start(bf16[512,24,128]{2,1,0:T(8,128)(2,1)} %param.3) | copy-start | bytes 9437188

commit v5 on v4

--- a/solution.py
+++ b/solution.py
@@ -59,31 +59,41 @@
 SHARE = {1: (0, 2), 2: (2, 1)}
 FAR = max(SHARE)
 TOP = 2 * NZ - 1
-KV1, QUERY, EXTRA, LAND = 1, 2, 3, 4
-RADIX = (5, 2, 8, 2, 2, 4, 2, 20, 20, 20)
+KV1, QUERY, EXTRA, LAND, HIGH = 1, 2, 3, 4, 20
+RADIX = (5, 2, 8, 2, 2, 4, 2, 21, 21, 21, 3)
 
 ORDER = (
-    ((0, 0, 5), (1, 7), (1, 0), (1, 1, 10), (1, 6, 1), (1, 2, 6), (2, 0, 2), (1, 5, 9), (1, 3, 7), (1, 4, 8)),
-    ((0, 1, 4, 6), (0, 0), (1, 6, 9), (1, 0), (1, 1, 1), (1, 2), (1, 3, 7), (1, 5), (1, 4, 12, 2, 8), (2, 1), (2, 0),
-     (3, 6, 19), (3, 0, 14), (3, 1), (4, 7, 3), (4, 0, 17), (4, 1), (4, 2), (4, 5), (4, 3, 15), (4, 6), (3, 2), (3, 3),
+    ((0, 0), (1, 7, 5, 20), (1, 0), (1, 1, 10), (1, 6), (1, 2, 1, 6), (2, 0, 2), (1, 5, 9), (1, 3, 7), (1, 4, 8)),
+    ((0, 1), (0, 0, 4, 6), (1, 6, 20), (1, 0), (1, 1, 9), (1, 2), (1, 5, 1), (1, 3, 7), (2, 1, 12, 2), (1, 4, 8), (2, 0),
+     (3, 6, 19), (3, 0, 14), (3, 1), (3, 2), (4, 7, 3, 17), (4, 0), (4, 1), (4, 2), (4, 3, 15), (4, 5), (4, 6), (3, 3),
      (4, 4, 16), (3, 4), (3, 5)),
-    ((0, 2, 5, 7), (0, 1), (1, 5, 8), (1, 1), (0, 0, 1, 4), (1, 0), (1, 2), (1, 3), (1, 4, 13, 15, 2), (2, 2), (2, 1),
-     (3, 5, 16, 18), (3, 1), (3, 2), (3, 3), (3, 4), (4, 1, 3), (4, 2), (4, 3), (4, 4), (4, 5), (4, 6), (4, 0, 12), (2, 0),
-     (3, 0), (4, 7, 19)),
-    ((0, 3, 6), (0, 2), (1, 4), (1, 2), (0, 1, 1, 5), (1, 1), (1, 3), (2, 3, 14, 2), (2, 2), (3, 4), (0, 0, 4), (1, 0), (3, 2),
-     (2, 1, 13), (3, 1), (3, 3), (2, 0, 12), (3, 0)),
+    ((0, 2), (0, 1, 5, 7), (1, 5, 20), (1, 1), (1, 2, 8), (0, 0, 4), (1, 0, 1), (1, 3), (1, 4), (2, 2, 13, 15, 2), (2, 1),
+     (3, 5), (3, 1), (2, 0, 16, 12), (3, 0), (3, 2), (3, 3, 18), (3, 4), (4, 7, 19, 3), (4, 0), (4, 1), (4, 2), (4, 3), (4, 4),
+     (4, 5), (4, 6)),
+    ((0, 3), (0, 2, 6), (1, 4, 20), (1, 2), (1, 3), (0, 1, 5), (1, 1, 1), (0, 0, 4), (1, 0), (2, 3, 2), (3, 4), (2, 2, 14),
+     (3, 2), (3, 3), (2, 1, 13), (3, 1), (2, 0, 12), (3, 0)),
 )
 
+
 def units(z):
+    work = list(ORDER[z])
+    if z > 0:
+        k = len(work)
+        while work[k - 1][0] == 3 and len(work[k - 1]) == 2 and len(work) - k < 3:
+            k -= 1
+        work = [(w, 0, SHARE[z][1] if w[0] == SHIFT else GQ) for w in work[:k]] + [
+            (w, h, 1) for h in range(GQ) for w in work[k:]]
+    else:
+        work = [(w, 0, GQ) for w in work]
+    last = {(w[0], h): i for i, (w, h0, n) in enumerate(work) for h in range(h0, h0 + n)}
     out = []
     steps = 0
-    work = ORDER[z]
-    last = {u[0]: i for i, u in enumerate(work)}
-    for i, (qs, ch, *acts) in enumerate(work):
-        heads = SHARE[z][1] if qs == SHIFT else GQ
+    for i, ((qs, ch, *acts), h0, heads) in enumerate(work):
         diagonal = TOP if qs == SHIFT else z if qs % 2 == 0 else TOP - z
-        out.append((qs, 1 if qs == SHIFT else qs // 2, ch, int(ch == diagonal), int(last[qs] == i), heads, steps % 2,
-                    *acts, *[0] * (3 - len(acts))))
+        ends = [last[qs, h] == i for h in range(h0, h0 + heads)]
+        assert all(ends) or not any(ends)
+        out.append((qs, 1 if qs == SHIFT else qs // 2, ch, int(ch == diagonal), int(ends[0]), heads, steps % 2,
+                    *acts, *[0] * (3 - len(acts)), h0))
         steps += heads
     return out
 
@@ -191,8 +201,8 @@
                 for kind in kinds:
                     xlocal(g, kind, part).start()
 
-    def xwait(g, kinds):
-        for part in range(2):
+    def xwait(g, kinds, parts=(0, 1)):
+        for part in parts:
             for kind in kinds:
                 xlocal(g, kind, part).wait()
                 for p in range(1, NX):
@@ -239,13 +249,14 @@
             down(I(g), ch)
         up(I(g), z)
         if g == 1:
-            up(I(g), TOP - z)
+            pl.when(z != 1)(lambda: up(I(g), TOP - z))
 
     def before(f):
         @pl.loop(0, 3)
         def _(i):
             act = jnp.where(i == 0, f[7], jnp.where(i == 1, f[8], f[9]))
             pl.when(act == KV1)(lambda: begin(1))
+            pl.when(act == HIGH)(lambda: xwait(0, (2,), (1,)))
 
             @pl.when(act == QUERY)
             def _():
@@ -261,7 +272,7 @@
                 for zz in SHARE:
                     pl.when(z == zz)(lambda: shift(zz).wait_recv())
 
-            @pl.when(act >= LAND)
+            @pl.when((act >= LAND) & (act < HIGH))
             def _():
                 g = lax.div(act - LAND, I(2 * NZ))
                 ch = lax.rem(jnp.maximum(act - LAND, 0), I(2 * NZ))
@@ -272,6 +283,7 @@
                     for d in zcopies(g, ch, 1, usend):
                         d.wait_recv()
                     up(g, ch)
+                    pl.when((z == 1) & (g == 1) & (ch == 0))(lambda: up(I(1), TOP - z))
 
                 @pl.when(source > z)
                 def _():
@@ -335,9 +347,8 @@
         sx, xx = bufs[par]
         return qb[f[0], h, pl.ds(e * tq, tq), :], kb.at[f[1], f[2]], sx.at[e], xx.at[e], e * tq if masked else None, rows
 
-    def step(fn, hn, f, h):
+    def step(fn, hn, f, h, parity):
         qs = f[0]
-        parity = lax.rem(f[6] + h, I(2))
         for par in range(2):
             for m_cur in (False, True):
                 for m_nxt in (False, True):
@@ -352,10 +363,10 @@
 
     first = fields(I(0))
     begin(0)
-    xwait(0, (2,))
+    xwait(0, (2,), (0,))
     before(first)
     for e in range(tiles):
-        stage(c, nxt(first, 0, e, 0, True), None)
+        stage(c, nxt(first, I(0), e, 0, True), None)
 
     @pl.loop(0, count)
     def _(u):
@@ -368,8 +379,10 @@
         def _(h):
             wrap = h == f[5] - 1
             pl.when(wrap & (u + 1 < count))(lambda: before(fn))
-            step([jnp.where(wrap, p, q) for p, q in zip(fn, f)], jnp.where(wrap, 0, h + 1), f, h)
-            after(f, h, [jnp.where(h == 0, p, q) for p, q in zip(w, f)], jnp.where(h == 0, w[5] - 1, h - 1))
+            step([jnp.where(wrap, p, q) for p, q in zip(fn, f)], jnp.where(wrap, fn[10], f[10] + h + 1), f, f[10] + h,
+                 lax.rem(f[6] + h, I(2)))
+            after(f, f[10] + h, [jnp.where(h == 0, p, q) for p, q in zip(w, f)],
+                  jnp.where(h == 0, w[10] + w[5] - 1, f[10] + h - 1))
 
     for g in range(SLOTS):
         for part in range(2):
@@ -378,7 +391,7 @@
                     xcopy(g, kind, part, p, j, mod(j + p)).wait_send()
     end = fields(count - 1)
     for e in range(tiles):
-        give_back(end[0], tiles * (end[5] - 1) + e)
+        give_back(end[0], tiles * (end[10] + end[5] - 1) + e)
     for g in range(SLOTS):
         for s in range(NZ):
             @pl.when(goes_down(g) & (s >= z))
@@ -468,7 +481,7 @@
                 dma((4, NX)),
             ],
             compiler_params=pltpu.CompilerParams(
-                collective_id=0, has_side_effects=True, vmem_limit_bytes=56 * 2**20),
+                collective_id=0, has_side_effects=True, vmem_limit_bytes=38 * 2**20),
         )(jnp.transpose(q, (1, 0, 2)), jnp.transpose(k, (1, 0, 2)), jnp.transpose(v, (1, 2, 0)))
         return jnp.transpose(ot, (1, 0, 2))
 

time: 153 us -> 145 us (0.948)
  Pallas kernels: 140 us -> 135 us
  local copies, waits for them, and re-layouts: 12.9 us -> 9.24 us
    pallas_call x1, Pallas kernels: 140 us -> 135 us  [local(): pl.pallas_call(functools.partial(kernel, c), out_shape=jax.ShapeDtypeStru...]
    transpose x1, local copies, waits for them, and re-layouts: 5.58 us -> 3.69 us  [local(): return jnp.transpose(ot, (1, 0, 2))]
    unnamed x5 -> x3, local copies, waits for them, and re-layouts: 7.29 us -> 5.55 us
where the time goes in v5:
time: 145 us
  Pallas kernels  135 us (93%)
  local copies, waits for them, and re-layouts  9.24 us (6%)
    pallas_call x1, Pallas kernels, local(): pl.pallas_call(functools.partial(kernel, c), out_shape=jax.ShapeDtypeStru...  135 us
    unnamed x3, local copies, waits for them, and re-layouts  5.55 us
    transpose x1, local copies, waits for them, and re-layouts, local(): return jnp.transpose(ot, (1, 0, 2))  3.69 us

profile of v5, /device:TPU:0, one launch (start us, length us, event | category | flops | bytes accessed | tf_op | source)
XLA Modules:
  0.0 144.5 jit_solution(5334588706565041649)
XLA Ops:
  0.0 1.4 copy.11
  1.4 1.6 %copy.6 = bf16[512,8,128]{0,2,1:T(8,128)(2,1)S(1)} copy(bf16[512,8,128]{2,1,0:T(8,128)(2,1)} %param.5) | data formatting | bytes 2097152 | tf_op args[2]
  3.0 2.6 %copy.10 = bf16[512,24,128]{2,0,1:T(8,128)(2,1)S(1)} copy(bf16[512,24,128]{2,1,0:T(8,128)(2,1)} %param.3) | data formatting | bytes 6291456 | tf_op args[0]
  5.6 135.2 %shard_map.37 = bf16[24,512,128]{2,1,0:T(8,128)(2,1)S(1)} custom-call(bf16[24,512,128]{2,1,0:T(8,128)(2,1)S(1)} %bitcast.9, bf16[8,512,128]{2,1,0:T(8,128)(2,1)S(1)} %bitcast.10, bf16[8,128,512]{2,1,0:T(8,128)(2,1)S(1)} %bitcast.11), custom_call_target="tpu_custom_call" | custom-call | tf_op jit(solution)/shard_map/pallas_call | solution.py:455
  140.8 3.7 %copy.7 = bf16[512,24,128]{2,1,0:T(8,128)(2,1)} copy(bf16[512,24,128]{2,0,1:T(8,128)(2,1)S(1)} %bitcast.8) | data formatting | bytes 6291456 | tf_op jit(solution)/shard_map/transpose | solution.py:486

commit v6 on v5

--- a/solution.py
+++ b/solution.py
@@ -62,21 +62,100 @@
 KV1, QUERY, EXTRA, LAND, HIGH = 1, 2, 3, 4, 20
 RADIX = (5, 2, 8, 2, 2, 4, 2, 21, 21, 21, 3)
 
-ORDER = (
-    ((0, 0), (1, 7, 5, 20), (1, 0), (1, 1, 10), (1, 6), (1, 2, 1, 6), (2, 0, 2), (1, 5, 9), (1, 3, 7), (1, 4, 8)),
-    ((0, 1), (0, 0, 4, 6), (1, 6, 20), (1, 0), (1, 1, 9), (1, 2), (1, 5, 1), (1, 3, 7), (2, 1, 12, 2), (1, 4, 8), (2, 0),
-     (3, 6, 19), (3, 0, 14), (3, 1), (3, 2), (4, 7, 3, 17), (4, 0), (4, 1), (4, 2), (4, 3, 15), (4, 5), (4, 6), (3, 3),
-     (4, 4, 16), (3, 4), (3, 5)),
-    ((0, 2), (0, 1, 5, 7), (1, 5, 20), (1, 1), (1, 2, 8), (0, 0, 4), (1, 0, 1), (1, 3), (1, 4), (2, 2, 13, 15, 2), (2, 1),
-     (3, 5), (3, 1), (2, 0, 16, 12), (3, 0), (3, 2), (3, 3, 18), (3, 4), (4, 7, 19, 3), (4, 0), (4, 1), (4, 2), (4, 3), (4, 4),
-     (4, 5), (4, 6)),
-    ((0, 3), (0, 2, 6), (1, 4, 20), (1, 2), (1, 3), (0, 1, 5), (1, 1, 1), (0, 0, 4), (1, 0), (2, 3, 2), (3, 4), (2, 2, 14),
-     (3, 2), (3, 3), (2, 1, 13), (3, 1), (2, 0, 12), (3, 0)),
-)
+LOW_KV, HIGH_KV, LOW_Q, HIGH_Q, KV1_HERE, Q1_HERE = 9.5, 15, 24, 32, 43, 60
+CHUNK, HOP, STEP = 11.25, 1.5, 1.28
+
+
+def slot(qs):
+    return 1 if qs == SHIFT else qs // 2
+
+
+def diagonal(z, qs):
+    return TOP if qs == SHIFT else z if qs % 2 == 0 else TOP - z
+
+
+def plan():
+    free, shifted, out, pend = {}, {}, [[] for _ in range(NZ)], [[] for _ in range(NZ)]
+    landing = [{} for _ in range(NZ)]
+    got = [set() for _ in range(NZ)]
+    done = [set() for _ in range(NZ)]
+    now = [LOW_Q] * NZ
+    todo = []
+
+    def wire(link, t, dur):
+        free[link] = max(t, free.get(link, 0)) + dur
+        return free[link] + HOP
+
+    def travel(z, g, ch, t, dz):
+        if dz < 0 and z > g or dz > 0 and z < (NZ - 1 if ch < NZ else FAR):
+            landing[z + dz][g, ch] = wire((dz, z), t, CHUNK)
+
+    def begin(z, g, low, high):
+        for ch, t in ((z, low), (TOP - z, high)):
+            got[z].add((g, ch))
+            travel(z, g, ch, t, -1)
+        travel(z, g, z, low, 1)
+        if g == 1 and z != 1:
+            travel(z, g, TOP - z, high, 1)
+
+    def act(z, a, t):
+        pend[z].append(a)
+        done[z].add(a)
+        if a == KV1:
+            begin(z, 1, t, t)
+        elif a == QUERY and z == 0:
+            for zz, (_, heads) in SHARE.items():
+                shifted[zz] = wire((1, 0), t, CHUNK * heads / 2) + 8 * (zz - 1)
+        elif LAND <= a < HIGH:
+            g, ch = (a - LAND) // (2 * NZ), (a - LAND) % (2 * NZ)
+            got[z].add((g, ch))
+            travel(z, g, ch, t, 1 if min(ch, TOP - ch) < z else -1)
+            if z == 1 and (g, ch) == (1, 0):
+                travel(z, 1, TOP - z, t, 1)
+
+    def waiting(z):
+        p = [(t, LAND + 2 * NZ * g + ch) for (g, ch), t in landing[z].items() if (g, ch) not in got[z]]
+        p += [(t, a) for a, t in ((HIGH, HIGH_Q), (KV1, KV1_HERE)) if a not in done[z]]
+        if KV1 in done[z] and QUERY not in done[z]:
+            p.append((Q1_HERE, QUERY))
+        if z in shifted and EXTRA not in done[z]:
+            p.append((shifted[z], EXTRA))
+        return sorted(p)
+
+    def ready(z, qs, ch):
+        need = {1: HIGH, 2: QUERY, 3: QUERY, SHIFT: EXTRA}.get(qs)
+        return (need is None or need in done[z]) and (slot(qs), ch) in got[z]
+
+    for z in range(NZ):
+        sets = [0, 1, 2] + [3] * (z > 0) + [SHIFT] * (z in SHARE)
+        todo.append([(qs, ch) for qs in sets for ch in range(diagonal(z, qs) + 1)])
+        begin(z, 0, LOW_KV, HIGH_KV)
+    while any(todo):
+        z = min((z for z in range(NZ) if todo[z]), key=lambda z: now[z])
+        for t, a in waiting(z):
+            if t <= now[z] and len(pend[z]) < 3:
+                act(z, a, now[z])
+        can = [u for u in todo[z] if ready(z, *u)]
+        if can:
+            rank = (0, 2, 1, 4, 3) if z == 0 else (0, 1, 3, 4, 2)
+            qs, ch = min(can, key=lambda u: (rank[u[0]], u[1] != diagonal(z, u[0]), u[1] if u[1] < diagonal(z, u[0]) else -u[1]))
+            todo[z].remove((qs, ch))
+            out[z].append((qs, ch, *pend[z]))
+            pend[z] = []
+            now[z] += STEP * (SHARE[z][1] if qs == SHIFT else GQ)
+        else:
+            coming = waiting(z)
+            if coming and len(pend[z]) < 3:
+                now[z] = max(now[z], coming[0][0])
+                act(z, coming[0][1], now[z])
+            else:
+                now[z] += 0.5
+    assert not any(pend)
+    return out, now
 
 
 def units(z):
-    work = list(ORDER[z])
+    work = plan()[0][z]
     if z > 0:
         k = len(work)
         while work[k - 1][0] == 3 and len(work[k - 1]) == 2 and len(work) - k < 3:
@@ -89,10 +168,9 @@
     out = []
     steps = 0
     for i, ((qs, ch, *acts), h0, heads) in enumerate(work):
-        diagonal = TOP if qs == SHIFT else z if qs % 2 == 0 else TOP - z
         ends = [last[qs, h] == i for h in range(h0, h0 + heads)]
         assert all(ends) or not any(ends)
-        out.append((qs, 1 if qs == SHIFT else qs // 2, ch, int(ch == diagonal), int(ends[0]), heads, steps % 2,
+        out.append((qs, slot(qs), ch, int(ch == diagonal(z, qs)), int(ends[0]), heads, steps % 2,
                     *acts, *[0] * (3 - len(acts)), h0))
         steps += heads
     return out
@@ -244,10 +322,11 @@
         a[i] = jnp.zeros(a.shape[1:], a.dtype)
 
     def begin(g):
-        xwait(g, (0, 1))
-        for ch in (z, TOP - z):
-            down(I(g), ch)
+        xwait(g, (0, 1), (0,))
+        down(I(g), z)
         up(I(g), z)
+        xwait(g, (0, 1), (1,))
+        down(I(g), TOP - z)
         if g == 1:
             pl.when(z != 1)(lambda: up(I(g), TOP - z))
 

time: 145 us -> 144 us (level)
  no operation moved by 1% of the time
where the time goes in v6:
time: 144 us; the launch traced here: 143 us
  Pallas kernels  134 us (93%)
  local copies, waits for them, and re-layouts  9.24 us (6%)
    pallas_call x1, Pallas kernels, local(): pl.pallas_call(functools.partial(kernel, c), out_shape=jax.ShapeDtypeStru...  134 us
    unnamed x3, local copies, waits for them, and re-layouts  5.55 us
    transpose x1, local copies, waits for them, and re-layouts, local(): return jnp.transpose(ot, (1, 0, 2))  3.69 us

profile of v6, /device:TPU:0, one launch (start us, length us, event | category | flops | bytes accessed | tf_op | source)
XLA Modules:
  0.0 143.3 jit_solution(18137407042735426995)
XLA Ops:
  0.0 1.4 copy.11
  1.4 1.6 %copy.6 = bf16[512,8,128]{0,2,1:T(8,128)(2,1)S(1)} copy(bf16[512,8,128]{2,1,0:T(8,128)(2,1)} %param.5) | data formatting | bytes 2097152 | tf_op args[2]
  3.0 2.6 %copy.10 = bf16[512,24,128]{2,0,1:T(8,128)(2,1)S(1)} copy(bf16[512,24,128]{2,1,0:T(8,128)(2,1)} %param.3) | data formatting | bytes 6291456 | tf_op args[0]
  5.6 134.1 %shard_map.37 = bf16[24,512,128]{2,1,0:T(8,128)(2,1)S(1)} custom-call(bf16[24,512,128]{2,1,0:T(8,128)(2,1)S(1)} %bitcast.9, bf16[8,512,128]{2,1,0:T(8,128)(2,1)S(1)} %bitcast.10, bf16[8,128,512]{2,1,0:T(8,128)(2,1)S(1)} %bitcast.11), custom_call_target="tpu_custom_call" | custom-call | tf_op jit(solution)/shard_map/pallas_call | solution.py:534
  139.6 3.7 %copy.7 = bf16[512,24,128]{2,1,0:T(8,128)(2,1)} copy(bf16[512,24,128]{2,0,1:T(8,128)(2,1)S(1)} %bitcast.8) | data formatting | bytes 6291456 | tf_op jit(solution)/shard_map/transpose | solution.py:565

commit v7 on v6

--- a/solution.py
+++ b/solution.py
@@ -62,8 +62,8 @@
 KV1, QUERY, EXTRA, LAND, HIGH = 1, 2, 3, 4, 20
 RADIX = (5, 2, 8, 2, 2, 4, 2, 21, 21, 21, 3)
 
-LOW_KV, HIGH_KV, LOW_Q, HIGH_Q, KV1_HERE, Q1_HERE = 9.5, 15, 24, 32, 43, 60
-CHUNK, HOP, STEP = 11.25, 1.5, 1.28
+LOW_KV, HIGH_KV, LOW_Q, HIGH_Q, KV1_HERE, Q1_HERE = 11, 17, 27, 36, 48, 66
+CHUNK, HOP, STEP = 12, 3, 1.4
 
 
 def slot(qs):

time: 144 us -> 141 us (0.979)
  Pallas kernels: 134 us -> 130 us
    pallas_call x1, Pallas kernels: 134 us -> 130 us  [local(): pl.pallas_call(functools.partial(kernel, c), out_shape=jax.ShapeDtypeStru...]
where the time goes in v7:
time: 141 us; the launch traced here: 139 us
  Pallas kernels  130 us (92%)
  local copies, waits for them, and re-layouts  9.24 us (7%)
    pallas_call x1, Pallas kernels, local(): pl.pallas_call(functools.partial(kernel, c), out_shape=jax.ShapeDtypeStru...  130 us
    unnamed x3, local copies, waits for them, and re-layouts  5.55 us
    transpose x1, local copies, waits for them, and re-layouts, local(): return jnp.transpose(ot, (1, 0, 2))  3.69 us

profile of v7, /device:TPU:0, one launch (start us, length us, event | category | flops | bytes accessed | tf_op | source)
XLA Modules:
  0.0 139.3 jit_solution(1225803999398358791)
XLA Ops:
  0.0 1.4 copy.11
  1.4 1.6 %copy.6 = bf16[512,8,128]{0,2,1:T(8,128)(2,1)S(1)} copy(bf16[512,8,128]{2,1,0:T(8,128)(2,1)} %param.5) | data formatting | bytes 2097152 | tf_op args[2]
  3.0 2.6 %copy.10 = bf16[512,24,128]{2,0,1:T(8,128)(2,1)S(1)} copy(bf16[512,24,128]{2,1,0:T(8,128)(2,1)} %param.3) | data formatting | bytes 6291456 | tf_op args[0]
  5.6 130.0 %shard_map.37 = bf16[24,512,128]{2,1,0:T(8,128)(2,1)S(1)} custom-call(bf16[24,512,128]{2,1,0:T(8,128)(2,1)S(1)} %bitcast.9, bf16[8,512,128]{2,1,0:T(8,128)(2,1)S(1)} %bitcast.10, bf16[8,128,512]{2,1,0:T(8,128)(2,1)S(1)} %bitcast.11), custom_call_target="tpu_custom_call" | custom-call | tf_op jit(solution)/shard_map/pallas_call | solution.py:534
  135.6 3.7 %copy.7 = bf16[512,24,128]{2,1,0:T(8,128)(2,1)} copy(bf16[512,24,128]{2,0,1:T(8,128)(2,1)S(1)} %bitcast.8) | data formatting | bytes 6291456 | tf_op jit(solution)/shard_map/transpose | solution.py:565
